TPU v7x, 32 devices: a whole 2x2x4 slice. The times are simulated.
32 devices in a mesh: dp: 32 (over z, y, x, core).
Axes of the slice: x: 2, y: 2, z: 4, core: 2. Of those that a mesh axis runs over, the one named last changes fastest.
Arguments:
- g_mat: bfloat16 [32, 9830400], P('dp')
- g_vec: bfloat16 [32, 16640], P('dp')
- p_mat: float32 [9830400], P('dp')
- m_mat: float32 [9830400], P('dp')
- v_mat: float32 [9830400], P('dp')
- p_vec: float32 [16640], replicated
- m_vec: float32 [16640], replicated
- v_vec: float32 [16640], replicated
- learn_rate: float32 [], replicated
Outputs:
- output 1: float32 [9830400], P('dp')
- output 2: float32 [9830400], P('dp')
- output 3: float32 [9830400], P('dp')
- output 4: float32 [16640], replicated
- output 5: float32 [16640], replicated
- output 6: float32 [16640], replicated
- output 7: bfloat16 [9830400], replicated
All inputs are finite; a program needn't handle non-finite values.
Results may differ from a plain program's by a relative error of at most 0.001.
Values are sent between devices in bfloat16 or wider.
A program may use at most 1 GiB of HBM per device.

v0:
```python
import jax
import jax.numpy as jnp
from jax import lax
from jax.sharding import PartitionSpec as P

STEP = 10
ADAM_BETA1 = 0.9
ADAM_BETA2 = 0.98
ADAM_EPS = 1e-8
WEIGHT_DECAY = 0.01
MAX_NORM = 1.0
NORM_EPS = 1e-6
BIAS_ONE = 1.0 - ADAM_BETA1 ** STEP
BIAS_TWO = 1.0 - ADAM_BETA2 ** STEP


def adam_update(grad_vals, param_vals, moment_one, moment_two, learn_rate, decay_rate):
    new_one = ADAM_BETA1 * moment_one + (1.0 - ADAM_BETA1) * grad_vals
    new_two = ADAM_BETA2 * moment_two + (1.0 - ADAM_BETA2) * grad_vals * grad_vals
    direction = (new_one / BIAS_ONE) / (jnp.sqrt(new_two / BIAS_TWO) + ADAM_EPS)
    return param_vals - learn_rate * (direction + decay_rate * param_vals), new_one, new_two


def solution(mesh):
    axis_name = mesh.axis_names[0]
    group_size = mesh.shape[axis_name]

    def local_step(g_mat, g_vec, p_mat, m_mat, v_mat, p_vec, m_vec, v_vec, learn_rate):
        send_rows = g_mat.reshape(group_size, -1)
        recv_rows = lax.all_to_all(send_rows, axis_name, 0, 0, tiled=True)
        grad_mat = jnp.sum(recv_rows.astype(jnp.float32), axis=0) / group_size
        grad_vec = lax.psum(g_vec[0].astype(jnp.float32), axis_name) / group_size
        norm_sq = lax.psum(jnp.sum(grad_mat * grad_mat), axis_name) + jnp.sum(grad_vec * grad_vec)
        clip_scale = jnp.minimum(1.0, MAX_NORM / (jnp.sqrt(norm_sq) + NORM_EPS))
        new_p_mat, new_m_mat, new_v_mat = adam_update(grad_mat * clip_scale, p_mat, m_mat, v_mat, learn_rate, WEIGHT_DECAY)
        new_p_vec, new_m_vec, new_v_vec = adam_update(grad_vec * clip_scale, p_vec, m_vec, v_vec, learn_rate, 0.0)
        full_params = lax.all_gather(new_p_mat.astype(jnp.bfloat16), axis_name, tiled=True)
        return new_p_mat, new_m_mat, new_v_mat, new_p_vec, new_m_vec, new_v_vec, full_params

    return jax.shard_map(
        local_step,
        mesh=mesh,
        in_specs=(P(axis_name, None), P(axis_name, None), P(axis_name), P(axis_name), P(axis_name), P(), P(), P(), P()),
        out_specs=(P(axis_name), P(axis_name), P(axis_name), P(), P(), P(), P()),
        check_vma=False,
    )
```

profile of v0, /device:TPU:0, one launch (start us, length us, event | category | flops | bytes accessed | tf_op | source)
XLA Modules:
  0.0 878.2 jit_solution(8060528360135426315)
XLA Ops:
  7.2 0.5 broadcast.9
  7.7 124.2 %reduce.3 = bf16[32,307200]{1,0:T(8,128)(2,1)} reduce(bf16[32,1,307200]{2,1,0:T(2,128)(2,1)} %bitcast.1, bf16[]{:T(256)} %broadcast.9), dimensions={1}, to_apply=%bitcast.reduce_sub_computation | reduce | bytes 39321600 | tf_op jit(solution)/shard_map/all_to_all | solution.py:30
  131.8 36.7 %reshape.23 = bf16[32,2,153600]{2,1,0:T(2,128)(2,1)} reshape(bf16[32,307200]{1,0:T(8,128)(2,1)} %reduce.3) | data formatting | bytes 39321600
  168.5 7.5 all-to-all-start
  176.0 0.0 all-reduce.2.cloned.1.call-start
  176.1 0.0 copy-done.5
  176.1 0.8 convert_reduce_fusion.1
  176.9 0.0 all-reduce.2.cloned.1.call-update
  176.9 0.2 all-gather.2.cloned.1.call-start
  177.8 407.4 %all-to-all-done = bf16[32,2,153600]{2,1,0:T(2,128)(2,1)} async-done(((bf16[32,2,153600]{2,1,0:T(2,128)(2,1)}), bf16[32,2,153600]{2,1,0:T(2,128)(2,1)}, u32[]{:S(2)}, u32[]{:S(2)}) %all-to-all-start) | async-done | bytes 19660832 | tf_op jit(solution)/shard_map/all_to_all | solution.py:30
  585.2 34.2 %reshape.24 = bf16[32,1,307200]{2,1,0:T(2,128)(2,1)} reshape(bf16[32,2,153600]{2,1,0:T(2,128)(2,1)} %all-to-all-done) | data formatting | bytes 39321600
  619.4 37.9 %convert_reduce_fusion = f32[307200]{0:T(1024)S(1)} fusion(bf16[32,1,307200]{2,1,0:T(2,128)(2,1)} %reshape.24), kind=kLoop, calls=%fused_computation | loop fusion | flops 19353600 | bytes 20889600 | tf_op jit(solution)/shard_map/reduce_sum | solution.py:31
  657.4 0.0 copy-start
  657.4 0.9 multiply_reduce_fusion
  658.3 1.5 multiply_reduce_fusion.1
  659.8 60.9 %psum.14 = f32[]{:T(128)} all-reduce(f32[]{:T(128)} %multiply_reduce_fusion), channel_id=1, replica_groups=mesh['dp'=32] {'dp'}, use_global_device_ids=true, to_apply=%region_2.0 | all-reduce | flops 1 | bytes 8 | tf_op jit(solution)/shard_map/psum | solution.py:33
  722.1 0.0 copy-start.2
  722.1 0.0 copy-start.3
  722.1 0.0 copy-start.4
  722.1 4.4 fusion.2
  726.5 0.0 all-gather.2.cloned.1.call-update
  726.6 0.7 multiply_subtract_fusion.1
  727.3 127.7 %all-gather.2.cloned.1.call-done = bf16[9830400]{0:T(1024)(128)(2,1)} async-done(((bf16[307200]{0:T(1024)(128)(2,1)}), bf16[9830400]{0:T(1024)(128)(2,1)}) %all-gather.2.cloned.1.call-update) | async-done | bytes 19660816 | tf_op jit(solution)/shard_map/all_gather | solution.py:37
  855.0 16.4 %copy.19 = bf16[9830400]{0:T(1024)(128)(2,1)} copy(bf16[9830400]{0:T(1024)(128)(2,1)} %all-gather.2.cloned.1.call-done) | data formatting | bytes 39321600
  (8 shorter events, 0.0 us)
Async XLA Ops:
  168.5 7.5 copy-start.5
  168.5 416.7 %all-to-all-start = ((bf16[32,2,153600]{2,1,0:T(2,128)(2,1)}), bf16[32,2,153600]{2,1,0:T(2,128)(2,1)}, u32[]{:S(2)}, u32[]{:S(2)}) async-start(bf16[32,2,153600]{2,1,0:T(2,128)(2,1)} %reshape.23), calls=%async_computation | async-start | bytes 39321600 | tf_op jit(solution)/shard_map/all_to_all | solution.py:30
  176.0 482.3 %all-reduce.2.cloned.1.call-start = ((), (), s32[]{:S(2)}) async-start(), calls=%async_computation.1 | async-start | bytes 139264 | tf_op jit(solution)/shard_map/psum | solution.py:32
  176.9 678.1 %all-gather.2.cloned.1.call-start = ((), (), s32[]{:S(2)}) async-start(), calls=%async_computation.2 | async-start | bytes 20275200 | tf_op jit(solution)/shard_map/all_gather | solution.py:37
  657.4 64.7 %copy-start = (f32[307200]{0:T(1024)S(1)}, f32[307200]{0:T(1024)}, u32[]{:S(2)}) copy-start(f32[307200]{0:T(1024)} %param.11) | copy-start | bytes 3686404
  722.1 4.4 copy-start.1
  722.1 4.4 copy-start.2
  722.1 4.4 copy-start.3
  722.1 4.4 copy-start.4
Sparse Core Ops, SparseCore 0:
  183.0 229.4 all-reduce.1
  726.6 128.3 all-gather.1
where the time goes:
time: 880 us; the launch traced here: 878 us
  waiting for transfers between devices  535 us (61%)
  other arithmetic  170 us (19%)
  local copies, waits for them, and re-layouts  87.8 us (10%)
  blocking collectives  60.9 us (7%)
  between operations  16.2 us (2%)
    all_to_all x1, waiting for transfers between devices, local_step(): recv_rows = lax.all_to_all(send_rows, axis_name, 0, 0, tiled=True)  407 us
    all_gather x1, waiting for transfers between devices, local_step(): lax.all_gather(new_p_mat.astype(jnp.bfloat16), axis_name, tiled=True)  128 us
    all_to_all x1, other arithmetic, local_step(): recv_rows = lax.all_to_all(send_rows, axis_name, 0, 0, tiled=True)  124 us
    unnamed x15, local copies, waits for them, and re-layouts  87.3 us
    psum x1, blocking collectives, local_step(): lax.psum(jnp.sum(grad_mat * grad_mat), axis_name)  60.9 us
    reduce_sum x1, other arithmetic, local_step(): grad_mat = jnp.sum(recv_rows.astype(jnp.float32), axis=0) / group_size  37.9 us
  transfers between devices with their start and end apart: 3, of which 2 were waited for; matrix products, arithmetic and copies ran while one was open for 8% of the time, Pallas kernels for 0%

commit v1 on v0

v1 whole, which is shorter than its diff:
```python
import jax
import jax.numpy as jnp
from jax import lax
from jax.experimental import pallas as pl
from jax.experimental.pallas import tpu as pltpu
from jax.sharding import PartitionSpec as P

STEP = 10
ADAM_BETA1 = 0.9
ADAM_BETA2 = 0.98
ADAM_EPS = 1e-8
WEIGHT_DECAY = 0.01
MAX_NORM = 1.0
NORM_EPS = 1e-6
BIAS_ONE = 1.0 - ADAM_BETA1 ** STEP
BIAS_TWO = 1.0 - ADAM_BETA2 ** STEP

DP = 32
PIECE = 2400
CHUNKS = 15
ROWS = PIECE // CHUNKS
HALF = ROWS // 2
RAB = 32
RCD = HALF - RAB
VEC = 130
VPAD = 136
MESH = pl.DeviceIdType.MESH
F32 = jnp.float32
BF16 = jnp.bfloat16


def adam_update(grad_vals, param_vals, moment_one, moment_two, learn_rate, decay_rate):
    new_one = ADAM_BETA1 * moment_one + (1.0 - ADAM_BETA1) * grad_vals
    new_two = ADAM_BETA2 * moment_two + (1.0 - ADAM_BETA2) * grad_vals * grad_vals
    direction = (new_one / BIAS_ONE) / (jnp.sqrt(new_two / BIAS_TWO) + ADAM_EPS)
    return param_vals - learn_rate * (direction + decay_rate * param_vals), new_one, new_two


def kernel(g, gv, p, m, v, pv, mv, vv, lr,
           po, mo, vo, pvo, mvo, vvo, pb,
           stage, dense, pab, pcd, abz, er, cdr, abr, fr, gsum, ssq, clip, vs, vr, ns, nr,
           in_sem, pmv_sem, s0_send, s0_recv, rs_send, er_recv, cd_recv, ab_recv, f_recv,
           vec_send, vec_recv, norm_send, norm_recv,
           ag_send, ag_ab, ag_cd, ag_cd1, ag_ab2, ag_ab3, ag_cd3, ag_d2d):
    me = lax.axis_index("dp")
    c = me % 2
    x = (me // 2) % 2
    y = (me // 4) % 2
    z = me // 8

    def dev(zz, yy, xx, cc):
        return ((zz * 2 + yy) * 2 + xx) * 2 + cc

    partner = dev(z, y, x, 1 - c)
    xs = dev(z, y, 1 - x, c)
    xo = dev(z, y, 1 - x, 1 - c)
    ys = dev(z, 1 - y, x, c)
    yo = dev(z, 1 - y, x, 1 - c)
    up = dev((z + 1) % 4, y, x, c)
    down = dev((z + 3) % 4, y, x, c)
    z1 = dev(z + 1 - 2 * (z % 2), y, x, c)
    z2 = dev((z + 2) % 4, y, x, c)
    nlow = z >= 1
    nhigh = z <= 2

    def send(src, dst, ssem, rsem, to):
        pltpu.make_async_remote_copy(
            src_ref=src, dst_ref=dst, send_sem=ssem, recv_sem=rsem, device_id=(to,), device_id_type=MESH
        ).start()

    def wait(ref, sem):
        pltpu.make_async_copy(ref, ref, sem).wait()

    def fetch(k, slot):
        def one(d, carry):
            off = pl.multiple_of((d * PIECE + k * ROWS) * 128, 1024)
            pltpu.make_async_copy(g.at[0:1, pl.ds(off, ROWS * 128)], stage.at[slot, d], in_sem.at[slot]).start()
            return carry
        lax.fori_loop(0, DP, one, 0)

    fetch(0, 0)
    pltpu.make_async_copy(p, po, pmv_sem.at[0]).start()
    pltpu.make_async_copy(m, mo, pmv_sem.at[1]).start()
    pltpu.make_async_copy(v, vo, pmv_sem.at[2]).start()

    barrier = pltpu.get_barrier_semaphore()
    for nb in (partner, xs, xo, ys, yo, z2):
        pl.semaphore_signal(barrier, inc=1, device_id=(nb,), device_id_type=MESH)

    @pl.when(nhigh)
    def _():
        pl.semaphore_signal(barrier, inc=1, device_id=(up,), device_id_type=MESH)

    @pl.when(nlow)
    def _():
        pl.semaphore_signal(barrier, inc=1, device_id=(down,), device_id_type=MESH)

    vs[0, 0:128] = gv[0:1, 0:16384].astype(F32).reshape(128, 128)
    vs[0, 128:VPAD] = jnp.zeros((VPAD - 128, 128), F32)
    vs[0, 128:VEC] = gv[0:1, 16384:16640].astype(F32).reshape(2, 128)
    ssq[...] = jnp.zeros((8, 128), F32)

    mid = (z >= 1) & (z <= 2)

    @pl.when(mid)
    def _():
        pl.semaphore_wait(barrier, 8)

    @pl.when(jnp.logical_not(mid))
    def _():
        pl.semaphore_wait(barrier, 7)

    partners = (partner, xs, ys, z1, z2)

    def vec_step(j):
        if j > 0:
            wait(vr.at[j - 1], vec_recv.at[j - 1])
            vs[j] = vs[j - 1] + vr[j - 1]
        if j < 5:
            send(vs.at[j], vr.at[j], vec_send.at[j], vec_recv.at[j], partners[j])

    def rbuf(k, d, j):
        return pb.at[k // 4, (k // 2) % 2, k % 2, d, pl.ds(j * 8 * HALF, 8 * HALF)]

    def stage0(k):
        slot = k % 2
        dslot = k % 3

        @pl.when(k + 1 < CHUNKS)
        def _():
            fetch(k + 1, 1 - slot)

        @pl.when(k >= 3)
        def _():
            wait(dense.at[dslot, :, pl.ds(1, 3)], s0_send.at[dslot])

        wait(stage.at[slot], in_sem.at[slot])

        for d in range(2):
            for q in (3, 2, 1, 0):
                cc = (c, 1 - c, c, 1 - c)[q]
                far = q >= 2

                def conv(b, carry, d=d, q=q, cc=cc, far=far):
                    if d == 0:
                        piece = dev(b // 2, b % 2, 1 - x if far else x, cc)
                    else:
                        piece = dev(b // 2, 1 - y if far else y, b % 2, cc)
                    vals = stage[slot, piece, 0:1, d * HALF * 128:(d + 1) * HALF * 128].astype(F32)
                    row = pl.multiple_of(b * HALF, 16)
                    dense[dslot, d, q, pl.ds(row, HALF)] = vals.reshape(HALF, 128).astype(BF16)
                    return carry

                lax.fori_loop(0, 8, conv, 0)
                if q > 0:
                    to = ((partner, xs, xo), (partner, ys, yo))[d][q - 1]
                    send(dense.at[dslot, d, q], rbuf(k, d, q - 1), s0_send.at[dslot], s0_recv.at[k], to)

    def z_sends(k, t, bufs, recv, rsem):
        @pl.when(z <= t)
        def _():
            dest = 3 + z - t
            if t > 0:
                @pl.when(nlow)
                def _():
                    wait(recv.at[k, t - 1], rsem.at[k, t - 1])
                    bufs[k, dest] += recv[k, t - 1]
            send(bufs.at[k, dest], recv.at[k, t], rs_send.at[k], rsem.at[k, t], up)

        @pl.when(3 - z <= t)
        def _():
            dest = t - (3 - z)
            if t > 0:
                @pl.when(nhigh)
                def _():
                    old = 0 if t == 1 else t + 1
                    wait(recv.at[k, old], rsem.at[k, old])
                    bufs[k, dest] += recv[k, old]
            new = 0 if t == 0 else t + 2
            send(bufs.at[k, dest], recv.at[k, new], rs_send.at[k], rsem.at[k, new], down)

    def z_final(k, bufs, recv, rsem):
        @pl.when(nlow)
        def _():
            wait(recv.at[k, 2], rsem.at[k, 2])
            bufs[k, z] += recv[k, 2]

        @pl.when(nhigh)
        def _():
            wait(recv.at[k, 4], rsem.at[k, 4])
            bufs[k, z] += recv[k, 4]

    def stage1(k):
        dslot = k % 3
        wait(dense.at[dslot, :, pl.ds(1, 3)], s0_recv.at[k])
        for d in range(2):
            def add(b, carry, d=d):
                row = pl.multiple_of(b * HALF, 16)
                tot = dense[dslot, d, 0, pl.ds(row, HALF)].astype(F32)
                for j in range(3):
                    off = pl.multiple_of(j * 8 * HALF + b * HALF, 16)
                    tot = tot + pb[k // 4, (k // 2) % 2, k % 2, d, pl.ds(off, HALF)].astype(F32)
                pab[k, d, b % 2, b // 2] = tot[0:RAB]
                pcd[k, b // 2, d, b % 2] = tot[RAB:HALF]
                return carry
            lax.fori_loop(0, 8, add, 0)
        send(pab.at[k, 0, 1 - y], er.at[k, 0], rs_send.at[k], er_recv.at[k], ys)
        send(pab.at[k, 1, 1 - x], er.at[k, 1], rs_send.at[k], er_recv.at[k], xs)
        z_sends(k, 0, pcd, cdr, cd_recv)

    def stage2(k):
        z_sends(k, 1, pcd, cdr, cd_recv)
        wait(er.at[k], er_recv.at[k])
        for zz in range(4):
            abz[k, zz, 0] = pab[k, 0, y, zz] + er[k, 0, zz]
            abz[k, zz, 1] = pab[k, 1, x, zz] + er[k, 1, zz]
        z_sends(k, 0, abz, abr, ab_recv)

    def stage3(k):
        z_sends(k, 2, pcd, cdr, cd_recv)
        z_sends(k, 1, abz, abr, ab_recv)

    def stage4(k):
        z_final(k, pcd, cdr, cd_recv)
        send(pcd.at[k, z, 0, 1 - y], fr.at[k, 0], rs_send.at[k], f_recv.at[k], ys)
        send(pcd.at[k, z, 1, 1 - x], fr.at[k, 1], rs_send.at[k], f_recv.at[k], xs)
        z_sends(k, 2, abz, abr, ab_recv)

    def stage5(k):
        z_final(k, abz, abr, ab_recv)
        wait(fr.at[k], f_recv.at[k])
        base = pl.multiple_of(k * ROWS, 16)
        parts = (
            (0, RAB, abz[k, z, 0]),
            (RAB, RCD, pcd[k, z, 0, y] + fr[k, 0]),
            (HALF, RAB, abz[k, z, 1]),
            (HALF + RAB, RCD, pcd[k, z, 1, x] + fr[k, 1]),
        )
        acc = ssq[...]
        for off, num, val in parts:
            val = val * (1.0 / DP)
            gsum[pl.ds(base + off, num)] = val
            acc = acc + jnp.sum((val * val).reshape(num // 8, 8, 128), axis=0)
        ssq[...] = acc

    def rs_iter(i, carry):
        for s, fn in enumerate((stage0, stage1, stage2, stage3, stage4, stage5)):
            k = i - s

            @pl.when((k >= 0) & (k < CHUNKS))
            def _(fn=fn, k=k):
                fn(k)
        for j in range(6):
            @pl.when(i == 1 + 2 * j)
            def _(j=j):
                vec_step(j)
        return carry

    lax.fori_loop(0, CHUNKS + 5, rs_iter, 0)

    ns[0] = ssq[...]
    for j in range(5):
        send(ns.at[j], nr.at[j], norm_send.at[j], norm_recv.at[j], partners[j])
        wait(nr.at[j], norm_recv.at[j])
        ns[j + 1] = ns[j] + nr[j]
    gvec = vs[5, 0:VEC] * (1.0 / DP)
    norm_sq = jnp.full((8, 128), jnp.sum(ns[5]) + jnp.sum(gvec * gvec))
    clip[...] = jnp.minimum(1.0, MAX_NORM / (jnp.sqrt(norm_sq) + NORM_EPS))
    rate = lr[0, 0]

    wait(po, pmv_sem.at[0])
    wait(mo, pmv_sem.at[1])
    wait(vo, pmv_sem.at[2])

    def ag_rows(k, off, num):
        return pl.ds(pl.multiple_of(k * ROWS + off, 16), num)

    full = slice(None)

    def region(zz, yy, xx, rows):
        return pb.at[zz, yy, xx, c, rows]

    def push(ref, k, rsem, to):
        send(ref, ref, ag_send.at[k], rsem, to)

    def ag0(k):
        def upd(b, carry):
            rows = pl.ds(pl.multiple_of(k * ROWS + b * 32, 16), 32)
            new = adam_update(gsum[rows] * clip[0:1], po[rows], mo[rows], vo[rows], rate, WEIGHT_DECAY)
            po[rows], mo[rows], vo[rows] = new
            pb[z, y, x, c, rows] = new[0].astype(BF16)
            return carry
        lax.fori_loop(0, ROWS // 32, upd, 0)
        ab = ag_rows(k, 0, 2 * RAB)

        @pl.when(nhigh)
        def _():
            push(region(z, y, x, ab), k, ag_ab.at[k, 0, 0], up)

        @pl.when(nlow)
        def _():
            push(region(z, y, x, ab), k, ag_ab.at[k, 1, 0], down)

        push(region(z, y, x, ag_rows(k, 2 * RAB, RCD)), k, ag_cd1.at[k], ys)
        push(region(z, y, x, ag_rows(k, 2 * RAB + RCD, RCD)), k, ag_cd1.at[k], xs)

    def z_ab(k, t):
        ab = ag_rows(k, 0, 2 * RAB)
        one = region(0, 0, 0, ab)

        @pl.when(z - 1 - t >= 0)
        def _():
            wait(one, ag_ab.at[k, 0, t])
            if t < 2:
                @pl.when(nhigh)
                def _():
                    push(region(z - 1 - t, y, x, ab), k, ag_ab.at[k, 0, t + 1], up)

        @pl.when(z + 1 + t <= 3)
        def _():
            wait(one, ag_ab.at[k, 1, t])
            if t < 2:
                @pl.when(nlow)
                def _():
                    push(region(z + 1 + t, y, x, ab), k, ag_ab.at[k, 1, t + 1], down)

    def cd_push(k, zz, d, t, to):
        push(region(zz, full, x, ag_rows(k, 2 * RAB, RCD)), k, ag_cd.at[k, d, t], to)
        push(region(zz, y, full, ag_rows(k, 2 * RAB + RCD, RCD)), k, ag_cd.at[k, d, t], to)

    def z_cd(k, t):
        both = pb.at[0, 0, full, full, ag_rows(k, 2 * RAB, RCD)]

        @pl.when(z - 1 - t >= 0)
        def _():
            wait(both, ag_cd.at[k, 0, t])
            if t < 2:
                @pl.when(nhigh)
                def _():
                    cd_push(k, z - 1 - t, 0, t + 1, up)

        @pl.when(z + 1 + t <= 3)
        def _():
            wait(both, ag_cd.at[k, 1, t])
            if t < 2:
                @pl.when(nlow)
                def _():
                    cd_push(k, z + 1 + t, 1, t + 1, down)

    def ag1(k):
        wait(pb.at[0, 0, 0, full, ag_rows(k, 2 * RAB, RCD)], ag_cd1.at[k])

        @pl.when(nhigh)
        def _():
            cd_push(k, z, 0, 0, up)

        @pl.when(nlow)
        def _():
            cd_push(k, z, 1, 0, down)

        z_ab(k, 0)

    def ag2(k):
        z_ab(k, 1)
        z_cd(k, 0)

    def ag3(k):
        z_ab(k, 2)
        ra = ag_rows(k, 0, RAB)
        rb = ag_rows(k, RAB, RAB)
        push(region(full, y, x, ra), k, ag_ab2.at[k], ys)
        push(region(full, y, x, rb), k, ag_ab2.at[k], xs)
        push(region(full, y, x, ag_rows(k, 0, 2 * RAB)), k, ag_d2d.at[k], partner)
        z_cd(k, 1)

    def ag4(k):
        ra = ag_rows(k, 0, RAB)
        rb = ag_rows(k, RAB, RAB)
        rc = ag_rows(k, 2 * RAB, RCD)
        rd = ag_rows(k, 2 * RAB + RCD, RCD)
        wait(pb.at[0, 0, full, full, ag_rows(k, 0, 2 * RAB)], ag_ab2.at[k])
        push(region(full, full, x, ra), k, ag_ab3.at[k], xs)
        push(region(full, y, full, rb), k, ag_ab3.at[k], ys)
        push(region(full, 1 - y, x, ra), k, ag_d2d.at[k], partner)
        push(region(full, y, 1 - x, rb), k, ag_d2d.at[k], partner)
        z_cd(k, 2)
        push(region(full, full, x, rc), k, ag_cd3.at[k], xs)
        push(region(full, y, full, rd), k, ag_cd3.at[k], ys)
        push(region(full, full, x, rc), k, ag_d2d.at[k], partner)
        push(region(full, y, full, rd), k, ag_d2d.at[k], partner)

    def ag5(k):
        wait(pb.at[0, full, full, full, ag_rows(k, 0, 2 * RAB)], ag_ab3.at[k])
        push(region(full, full, 1 - x, ag_rows(k, 0, RAB)), k, ag_d2d.at[k], partner)
        push(region(full, 1 - y, full, ag_rows(k, RAB, RAB)), k, ag_d2d.at[k], partner)
        wait(pb.at[full, full, full, 0, ag_rows(k, 2 * RAB, RCD)], ag_cd3.at[k])
        push(region(full, full, 1 - x, ag_rows(k, 2 * RAB, RCD)), k, ag_d2d.at[k], partner)
        push(region(full, 1 - y, full, ag_rows(k, 2 * RAB + RCD, RCD)), k, ag_d2d.at[k], partner)

    def ag_iter(i, carry):
        for s, fn in enumerate((ag0, ag1, ag2, ag3, ag4, ag5)):
            k = i - s

            @pl.when((k >= 0) & (k < CHUNKS))
            def _(fn=fn, k=k):
                fn(k)
        return carry

    lax.fori_loop(0, CHUNKS + 5, ag_iter, 0)

    newv = adam_update(gvec * clip[0:1], pv[...], mv[...], vv[...], rate, 0.0)
    pvo[...], mvo[...], vvo[...] = newv

    def drain(k, carry):
        wait(pb.at[full, full, full, 0, ag_rows(k, 0, ROWS)], ag_d2d.at[k])
        @pl.when(mid)
        def _():
            wait(pb.at[0, 0, full, full, pl.ds(0, 1368)], ag_send.at[k])

        @pl.when(jnp.logical_not(mid))
        def _():
            wait(pb.at[0, 0, 0, full, pl.ds(0, 2224)], ag_send.at[k])

        wait(gsum.at[pl.ds(0, 1120)], rs_send.at[k])
        return carry

    lax.fori_loop(0, CHUNKS, drain, 0)
    for s in range(3):
        wait(dense.at[s, :, pl.ds(1, 3)], s0_send.at[s])
    for j in range(5):
        wait(vs.at[j], vec_send.at[j])
        wait(ns.at[j], norm_send.at[j])


def solution(mesh):
    axis_name = mesh.axis_names[0]
    vm = pl.BlockSpec(memory_space=pltpu.VMEM)
    hbm = pl.BlockSpec(memory_space=pl.ANY)
    dma = pltpu.SemaphoreType.DMA
    K = CHUNKS

    call = pl.pallas_call(
        kernel,
        name="adam_step",
        out_shape=(
            [pltpu.VMEM((PIECE, 128), F32)] * 3
            + [pltpu.VMEM((VEC, 128), F32)] * 3
            + [pltpu.VMEM((4, 2, 2, 2, PIECE, 128), BF16)]
        ),
        in_specs=[hbm, vm, hbm, hbm, hbm, vm, vm, vm, pl.BlockSpec(memory_space=pltpu.SMEM)],
        out_specs=[vm] * 7,
        scratch_shapes=[
            pltpu.VMEM((2, DP, 1, ROWS * 128), BF16),
            pltpu.VMEM((3, 2, 4, 8 * HALF, 128), BF16),
            pltpu.VMEM((K, 2, 2, 4, RAB, 128), F32),
            pltpu.VMEM((K, 4, 2, 2, RCD, 128), F32),
            pltpu.VMEM((K, 4, 2, RAB, 128), F32),
            pltpu.VMEM((K, 2, 4, RAB, 128), F32),
            pltpu.VMEM((K, 5, 2, 2, RCD, 128), F32),
            pltpu.VMEM((K, 5, 2, RAB, 128), F32),
            pltpu.VMEM((K, 2, RCD, 128), F32),
            pltpu.VMEM((PIECE, 128), F32),
            pltpu.VMEM((8, 128), F32),
            pltpu.VMEM((8, 128), F32),
            pltpu.VMEM((6, VPAD, 128), F32),
            pltpu.VMEM((5, VPAD, 128), F32),
            pltpu.VMEM((6, 8, 128), F32),
            pltpu.VMEM((5, 8, 128), F32),
            dma((2,)), dma((3,)), dma((3,)), dma((K,)), dma((K,)), dma((K,)), dma((K, 5)), dma((K, 5)), dma((K,)),
            dma((5,)), dma((5,)), dma((5,)), dma((5,)),
            dma((K,)), dma((K, 2, 3)), dma((K, 2, 3)), dma((K,)), dma((K,)), dma((K,)), dma((K,)), dma((K,)),
        ],
        compiler_params=pltpu.CompilerParams(
            collective_id=0, has_side_effects=True, vmem_limit_bytes=37 * 2 ** 20
        ),
    )

    def local_step(g_mat, g_vec, p_mat, m_mat, v_mat, p_vec, m_vec, v_vec, learn_rate):
        outs = call(
            g_mat, g_vec,
            p_mat.reshape(PIECE, 128), m_mat.reshape(PIECE, 128), v_mat.reshape(PIECE, 128),
            p_vec.reshape(VEC, 128), m_vec.reshape(VEC, 128), v_vec.reshape(VEC, 128),
            learn_rate.reshape(1, 1),
        )
        return tuple(o.reshape(-1) for o in outs)

    return jax.shard_map(
        local_step,
        mesh=mesh,
        in_specs=(P(axis_name, None), P(axis_name, None), P(axis_name), P(axis_name), P(axis_name), P(), P(), P(), P()),
        out_specs=(P(axis_name), P(axis_name), P(axis_name), P(), P(), P(), P()),
        check_vma=False,
    )
```

time: 880 us -> 270 us (0.31)
  waiting for transfers between devices: 535 us -> 0 us
  Pallas kernels: 0 us -> 257 us
  other arithmetic: 170 us -> 0 us
  local copies, waits for them, and re-layouts: 87.8 us -> 12.1 us
  blocking collectives: 60.9 us -> 0 us
  between operations: 16.2 us -> 1.29 us
    all_to_all x1 -> x0, waiting for transfers between devices: 407 us -> none  [local_step(): recv_rows = lax.all_to_all(send_rows, axis_name, 0, 0, tiled=True)]
    pallas_call x0 -> x1, Pallas kernels: none -> 257 us  [local_step(): call(g_mat, g_vec, p_mat.reshape(PIECE, 128), m_mat.reshape(PIECE, 128),...]
    all_gather x1 -> x0, waiting for transfers between devices: 128 us -> none  [local_step(): lax.all_gather(new_p_mat.astype(jnp.bfloat16), axis_name, tiled=True)]
    all_to_all x1 -> x0, other arithmetic: 124 us -> none  [local_step(): recv_rows = lax.all_to_all(send_rows, axis_name, 0, 0, tiled=True)]
    unnamed x15 -> x7, local copies, waits for them, and re-layouts: 87.3 us -> 12.1 us
    psum x1 -> x0, blocking collectives: 60.9 us -> none  [local_step(): lax.psum(jnp.sum(grad_mat * grad_mat), axis_name)]
    reduce_sum x3 -> x0, other arithmetic: 40.4 us -> none  [the longest x1 37.9 us: local_step(): grad_mat = jnp.sum(recv_rows.astype(jnp.float32), axis=0) / group_size]
  transfers between devices with their start and end apart: 3 -> 0, of which waited for: 2 -> 0; matrix products, arithmetic and copies ran while one was open for 8% -> 0% of each run, Pallas kernels for 0% -> 0%
where the time goes in v1:
time: 270 us
  Pallas kernels  257 us (95%)
  local copies, waits for them, and re-layouts  12.1 us (4%)
    pallas_call x1, Pallas kernels, local_step(): call(g_mat, g_vec, p_mat.reshape(PIECE, 128), m_mat.reshape(PIECE, 128),...  257 us
    unnamed x7, local copies, waits for them, and re-layouts  12.1 us

profile of v1, /device:TPU:0, one launch (start us, length us, event | category | flops | bytes accessed | tf_op | source)
XLA Modules:
  0.0 270.2 jit_solution(10763704553687801189)
XLA Ops:
  1.3 256.8 %adam_step.1 = (f32[2400,128]{1,0:T(8,128)S(1)}, f32[2400,128]{1,0:T(8,128)S(1)}, f32[2400,128]{1,0:T(8,128)S(1)}, f32[130,128]{1,0:T(8,128)S(1)}, f32[130,128]{...) custom-call(bf16[1,9830400]{1,0:T(2,128)(2,1)} %g.1, bf16[1,16640]{1,0:T(2,128)(2,1)} %gv.1, ...), custom_call_target="tpu_custom_call" | custom-call | tf_op jit(solution)/shard_map/adam_step/pallas_call | solution.py:479
  258.1 1.1 copy.23
  259.2 1.1 copy.24
  260.3 0.6 copy.26
  260.9 0.6 copy.27
  261.6 0.6 copy.28
  262.2 1.1 copy.25
  263.3 6.9 %copy.29 = bf16[9830400]{0:T(1024)(128)(2,1)} copy(bf16[9830400]{0:T(1024)(128)(2,1)S(1)} %bitcast.15) | data formatting | bytes 39321600

commit v2 on v1

--- a/solution.py
+++ b/solution.py
@@ -17,10 +17,10 @@
 
 DP = 32
 PIECE = 2400
-CHUNKS = 15
+CHUNKS = 25
 ROWS = PIECE // CHUNKS
 HALF = ROWS // 2
-RAB = 32
+RAB = 16
 RCD = HALF - RAB
 VEC = 130
 VPAD = 136
@@ -102,13 +102,14 @@
 
     mid = (z >= 1) & (z <= 2)
 
-    @pl.when(mid)
-    def _():
-        pl.semaphore_wait(barrier, 8)
-
-    @pl.when(jnp.logical_not(mid))
-    def _():
-        pl.semaphore_wait(barrier, 7)
+    def await_neighbours():
+        @pl.when(mid)
+        def _():
+            pl.semaphore_wait(barrier, 8)
+
+        @pl.when(jnp.logical_not(mid))
+        def _():
+            pl.semaphore_wait(barrier, 7)
 
     partners = (partner, xs, ys, z1, z2)
 
@@ -119,10 +120,19 @@
         if j < 5:
             send(vs.at[j], vr.at[j], vec_send.at[j], vec_recv.at[j], partners[j])
 
+    per = PIECE // (24 * HALF)
+
+    def rpiece(k, d):
+        at = (2 * k + d) // per
+        return at // 8, (at // 4) % 2, (at // 2) % 2, at % 2
+
+    def roff(k, d):
+        return ((2 * k + d) % per) * 24 * HALF
+
     def rbuf(k, d, j):
-        return pb.at[k // 4, (k // 2) % 2, k % 2, d, pl.ds(j * 8 * HALF, 8 * HALF)]
-
-    def stage0(k):
+        return pb.at[(*rpiece(k, d), pl.ds(roff(k, d) + j * 8 * HALF, 8 * HALF))]
+
+    def convert(k):
         slot = k % 2
         dslot = k % 3
 
@@ -136,25 +146,31 @@
 
         wait(stage.at[slot], in_sem.at[slot])
 
-        for d in range(2):
-            for q in (3, 2, 1, 0):
-                cc = (c, 1 - c, c, 1 - c)[q]
-                far = q >= 2
-
-                def conv(b, carry, d=d, q=q, cc=cc, far=far):
+        def conv(b, carry):
+            row = pl.multiple_of(b * HALF, 16)
+            for d in range(2):
+                for q in range(4):
+                    cc = 1 - c if q % 2 else c
                     if d == 0:
-                        piece = dev(b // 2, b % 2, 1 - x if far else x, cc)
+                        piece = dev(b // 2, b % 2, 1 - x if q >= 2 else x, cc)
                     else:
-                        piece = dev(b // 2, 1 - y if far else y, b % 2, cc)
+                        piece = dev(b // 2, 1 - y if q >= 2 else y, b % 2, cc)
                     vals = stage[slot, piece, 0:1, d * HALF * 128:(d + 1) * HALF * 128].astype(F32)
-                    row = pl.multiple_of(b * HALF, 16)
                     dense[dslot, d, q, pl.ds(row, HALF)] = vals.reshape(HALF, 128).astype(BF16)
-                    return carry
-
-                lax.fori_loop(0, 8, conv, 0)
-                if q > 0:
-                    to = ((partner, xs, xo), (partner, ys, yo))[d][q - 1]
-                    send(dense.at[dslot, d, q], rbuf(k, d, q - 1), s0_send.at[dslot], s0_recv.at[k], to)
+            return carry
+
+        lax.fori_loop(0, 8, conv, 0)
+
+    def stage0(k):
+        dslot = k % 3
+        for q in (3, 2, 1):
+            for d in range(2):
+                to = ((partner, xs, xo), (partner, ys, yo))[d][q - 1]
+                send(dense.at[dslot, d, q], rbuf(k, d, q - 1), s0_send.at[dslot], s0_recv.at[k], to)
+
+        @pl.when(k + 1 < CHUNKS)
+        def _():
+            convert(k + 1)
 
     def z_sends(k, t, bufs, recv, rsem):
         @pl.when(z <= t)
@@ -198,8 +214,8 @@
                 row = pl.multiple_of(b * HALF, 16)
                 tot = dense[dslot, d, 0, pl.ds(row, HALF)].astype(F32)
                 for j in range(3):
-                    off = pl.multiple_of(j * 8 * HALF + b * HALF, 16)
-                    tot = tot + pb[k // 4, (k // 2) % 2, k % 2, d, pl.ds(off, HALF)].astype(F32)
+                    off = pl.multiple_of(roff(k, d) + j * 8 * HALF + b * HALF, 16)
+                    tot = tot + pb[(*rpiece(k, d), pl.ds(off, HALF))].astype(F32)
                 pab[k, d, b % 2, b // 2] = tot[0:RAB]
                 pcd[k, b // 2, d, b % 2] = tot[RAB:HALF]
                 return carry
@@ -256,15 +272,21 @@
                 vec_step(j)
         return carry
 
+    convert(0)
+    await_neighbours()
     lax.fori_loop(0, CHUNKS + 5, rs_iter, 0)
 
-    ns[0] = ssq[...]
-    for j in range(5):
-        send(ns.at[j], nr.at[j], norm_send.at[j], norm_recv.at[j], partners[j])
-        wait(nr.at[j], norm_recv.at[j])
-        ns[j + 1] = ns[j] + nr[j]
+    ns[...] = jnp.sum(ssq[...], axis=0, keepdims=True)
+    nr[me] = ns[...]
+
+    def tell(j, carry):
+        send(ns, nr.at[me], norm_send, norm_recv, (me + j) % DP)
+        return carry
+
+    lax.fori_loop(1, DP, tell, 0)
+    wait(nr.at[pl.ds(0, DP - 1)], norm_recv)
     gvec = vs[5, 0:VEC] * (1.0 / DP)
-    norm_sq = jnp.full((8, 128), jnp.sum(ns[5]) + jnp.sum(gvec * gvec))
+    norm_sq = jnp.full((8, 128), jnp.sum(nr[...]) + jnp.sum(gvec * gvec))
     clip[...] = jnp.minimum(1.0, MAX_NORM / (jnp.sqrt(norm_sq) + NORM_EPS))
     rate = lr[0, 0]
 
@@ -413,15 +435,17 @@
 
     def drain(k, carry):
         wait(pb.at[full, full, full, 0, ag_rows(k, 0, ROWS)], ag_d2d.at[k])
+        base, along = 24 * RAB + 18 * RCD + 16 * ROWS, 2 * RAB + 4 * RCD
+
         @pl.when(mid)
         def _():
-            wait(pb.at[0, 0, full, full, pl.ds(0, 1368)], ag_send.at[k])
+            wait(pb.at[0, 0, full, full, pl.ds(0, (base + 5 * along) // 4)], ag_send.at[k])
 
         @pl.when(jnp.logical_not(mid))
         def _():
-            wait(pb.at[0, 0, 0, full, pl.ds(0, 2224)], ag_send.at[k])
-
-        wait(gsum.at[pl.ds(0, 1120)], rs_send.at[k])
+            wait(pb.at[0, 0, 0, full, pl.ds(0, (base + along) // 2)], ag_send.at[k])
+
+        wait(gsum.at[pl.ds(0, 14 * HALF)], rs_send.at[k])
         return carry
 
     lax.fori_loop(0, CHUNKS, drain, 0)
@@ -429,7 +453,17 @@
         wait(dense.at[s, :, pl.ds(1, 3)], s0_send.at[s])
     for j in range(5):
         wait(vs.at[j], vec_send.at[j])
-        wait(ns.at[j], norm_send.at[j])
+    wait(nr.at[pl.ds(0, DP - 1)], norm_send)
+
+
+def finish(*refs):
+    srcs, dsts, sem = refs[:7], refs[7:14], refs[14]
+    copies = [pltpu.make_async_copy(srcs[6].at[zz, yy], dsts[6].at[zz, yy], sem.at[6 + zz * 2 + yy]) for zz in range(4) for yy in range(2)]
+    copies += [pltpu.make_async_copy(srcs[i], dsts[i], sem.at[i]) for i in range(6)]
+    for copy in copies:
+        copy.start()
+    for copy in copies:
+        copy.wait()
 
 
 def solution(mesh):
@@ -464,15 +498,26 @@
             pltpu.VMEM((8, 128), F32),
             pltpu.VMEM((6, VPAD, 128), F32),
             pltpu.VMEM((5, VPAD, 128), F32),
-            pltpu.VMEM((6, 8, 128), F32),
-            pltpu.VMEM((5, 8, 128), F32),
+            pltpu.VMEM((1, 128), F32),
+            pltpu.VMEM((DP, 1, 128), F32),
             dma((2,)), dma((3,)), dma((3,)), dma((K,)), dma((K,)), dma((K,)), dma((K, 5)), dma((K, 5)), dma((K,)),
-            dma((5,)), dma((5,)), dma((5,)), dma((5,)),
+            dma((5,)), dma((5,)), dma, dma,
             dma((K,)), dma((K, 2, 3)), dma((K, 2, 3)), dma((K,)), dma((K,)), dma((K,)), dma((K,)), dma((K,)),
         ],
         compiler_params=pltpu.CompilerParams(
             collective_id=0, has_side_effects=True, vmem_limit_bytes=37 * 2 ** 20
         ),
+    )
+
+    shapes = [(PIECE, 128)] * 3 + [(VEC, 128)] * 3
+    copy_out = pl.pallas_call(
+        finish,
+        name="copy_out",
+        out_shape=[jax.ShapeDtypeStruct(s, F32) for s in shapes] + [jax.ShapeDtypeStruct((4, 2, 2, 2, PIECE, 128), BF16)],
+        in_specs=[vm] * 7,
+        out_specs=[hbm] * 7,
+        scratch_shapes=[dma((14,))],
+        compiler_params=pltpu.CompilerParams(vmem_limit_bytes=2 ** 20),
     )
 
     def local_step(g_mat, g_vec, p_mat, m_mat, v_mat, p_vec, m_vec, v_vec, learn_rate):
@@ -482,7 +527,7 @@
             p_vec.reshape(VEC, 128), m_vec.reshape(VEC, 128), v_vec.reshape(VEC, 128),
             learn_rate.reshape(1, 1),
         )
-        return tuple(o.reshape(-1) for o in outs)
+        return tuple(o.reshape(-1) for o in copy_out(*outs))
 
     return jax.shard_map(
         local_step,

time: 270 us -> 263 us (0.974)
  local copies, waits for them, and re-layouts: 12.1 us -> 0 us
  Pallas kernels: 257 us -> 261 us
    unnamed x7 -> x0, local copies, waits for them, and re-layouts: 12.1 us -> none
    pallas_call x0 -> x1, Pallas kernels: none -> 7.96 us  [local_step(): return tuple((o.reshape(-1) for o in copy_out(*outs)))]
    pallas_call x1, Pallas kernels: 257 us -> 253 us  [local_step(): call(g_mat, g_vec, p_mat.reshape(PIECE, 128), m_mat.reshape(PIECE, 128),...]
where the time goes in v2:
time: 263 us
  Pallas kernels  261 us (99%)
    pallas_call x1, Pallas kernels, local_step(): call(g_mat, g_vec, p_mat.reshape(PIECE, 128), m_mat.reshape(PIECE, 128),...  253 us
    pallas_call x1, Pallas kernels, local_step(): return tuple((o.reshape(-1) for o in copy_out(*outs)))  7.96 us

profile of v2, /device:TPU:0, one launch (start us, length us, event | category | flops | bytes accessed | tf_op | source)
XLA Modules:
  0.0 262.6 jit_solution(8206715617718327115)
XLA Ops:
  1.3 253.3 %adam_step.1 = (f32[2400,128]{1,0:T(8,128)S(1)}, f32[2400,128]{1,0:T(8,128)S(1)}, f32[2400,128]{1,0:T(8,128)S(1)}, f32[130,128]{1,0:T(8,128)S(1)}, f32[130,128]{...) custom-call(bf16[1,9830400]{1,0:T(2,128)(2,1)} %g.1, bf16[1,16640]{1,0:T(2,128)(2,1)} %gv.1, ...), custom_call_target="tpu_custom_call" | custom-call | tf_op jit(solution)/shard_map/adam_step/pallas_call | solution.py:524
  254.6 8.0 %copy_out.1 = (f32[2400,128]{1,0:T(8,128)}, f32[2400,128]{1,0:T(8,128)}, f32[2400,128]{1,0:T(8,128)}, f32[130,128]{1,0:T(8,128)}, f32[130,128]{1,0:T(8,128)}, /*...) custom-call(f32[2400,128]{1,0:T(8,128)S(1)} %get-tuple-element.21.refs_0_, ...), custom_call_target="tpu_custom_call" | custom-call | tf_op jit(solution)/shard_map/copy_out/pallas_call | solution.py:530

commit v3 on v2

--- a/solution.py
+++ b/solution.py
@@ -22,6 +22,8 @@
 HALF = ROWS // 2
 RAB = 16
 RCD = HALF - RAB
+SKEW_RS = 2
+SKEW_AG = 2
 VEC = 130
 VPAD = 136
 MESH = pl.DeviceIdType.MESH
@@ -134,13 +136,13 @@
 
     def convert(k):
         slot = k % 2
-        dslot = k % 3
+        dslot = k % 4
 
         @pl.when(k + 1 < CHUNKS)
         def _():
             fetch(k + 1, 1 - slot)
 
-        @pl.when(k >= 3)
+        @pl.when(k >= 4)
         def _():
             wait(dense.at[dslot, :, pl.ds(1, 3)], s0_send.at[dslot])
 
@@ -162,7 +164,7 @@
         lax.fori_loop(0, 8, conv, 0)
 
     def stage0(k):
-        dslot = k % 3
+        dslot = k % 4
         for q in (3, 2, 1):
             for d in range(2):
                 to = ((partner, xs, xo), (partner, ys, yo))[d][q - 1]
@@ -207,7 +209,7 @@
             bufs[k, z] += recv[k, 4]
 
     def stage1(k):
-        dslot = k % 3
+        dslot = k % 4
         wait(dense.at[dslot, :, pl.ds(1, 3)], s0_recv.at[k])
         for d in range(2):
             def add(b, carry, d=d):
@@ -261,7 +263,7 @@
 
     def rs_iter(i, carry):
         for s, fn in enumerate((stage0, stage1, stage2, stage3, stage4, stage5)):
-            k = i - s
+            k = i - SKEW_RS * s
 
             @pl.when((k >= 0) & (k < CHUNKS))
             def _(fn=fn, k=k):
@@ -274,7 +276,7 @@
 
     convert(0)
     await_neighbours()
-    lax.fori_loop(0, CHUNKS + 5, rs_iter, 0)
+    lax.fori_loop(0, CHUNKS + 5 * SKEW_RS, rs_iter, 0)
 
     ns[...] = jnp.sum(ssq[...], axis=0, keepdims=True)
     nr[me] = ns[...]
@@ -421,14 +423,14 @@
 
     def ag_iter(i, carry):
         for s, fn in enumerate((ag0, ag1, ag2, ag3, ag4, ag5)):
-            k = i - s
+            k = i - SKEW_AG * s
 
             @pl.when((k >= 0) & (k < CHUNKS))
             def _(fn=fn, k=k):
                 fn(k)
         return carry
 
-    lax.fori_loop(0, CHUNKS + 5, ag_iter, 0)
+    lax.fori_loop(0, CHUNKS + 5 * SKEW_AG, ag_iter, 0)
 
     newv = adam_update(gvec * clip[0:1], pv[...], mv[...], vv[...], rate, 0.0)
     pvo[...], mvo[...], vvo[...] = newv
@@ -449,7 +451,7 @@
         return carry
 
     lax.fori_loop(0, CHUNKS, drain, 0)
-    for s in range(3):
+    for s in range(4):
         wait(dense.at[s, :, pl.ds(1, 3)], s0_send.at[s])
     for j in range(5):
         wait(vs.at[j], vec_send.at[j])
@@ -485,7 +487,7 @@
         out_specs=[vm] * 7,
         scratch_shapes=[
             pltpu.VMEM((2, DP, 1, ROWS * 128), BF16),
-            pltpu.VMEM((3, 2, 4, 8 * HALF, 128), BF16),
+            pltpu.VMEM((4, 2, 4, 8 * HALF, 128), BF16),
             pltpu.VMEM((K, 2, 2, 4, RAB, 128), F32),
             pltpu.VMEM((K, 4, 2, 2, RCD, 128), F32),
             pltpu.VMEM((K, 4, 2, RAB, 128), F32),
@@ -500,7 +502,7 @@
             pltpu.VMEM((5, VPAD, 128), F32),
             pltpu.VMEM((1, 128), F32),
             pltpu.VMEM((DP, 1, 128), F32),
-            dma((2,)), dma((3,)), dma((3,)), dma((K,)), dma((K,)), dma((K,)), dma((K, 5)), dma((K, 5)), dma((K,)),
+            dma((2,)), dma((3,)), dma((4,)), dma((K,)), dma((K,)), dma((K,)), dma((K, 5)), dma((K, 5)), dma((K,)),
             dma((5,)), dma((5,)), dma, dma,
             dma((K,)), dma((K, 2, 3)), dma((K, 2, 3)), dma((K,)), dma((K,)), dma((K,)), dma((K,)), dma((K,)),
         ],

time: 263 us -> 261 us (level)
  no operation moved by 1% of the time
where the time goes in v3:
time: 261 us
  Pallas kernels  260 us (100%)
    pallas_call x1, Pallas kernels, local_step(): call(g_mat, g_vec, p_mat.reshape(PIECE, 128), m_mat.reshape(PIECE, 128),...  252 us
    pallas_call x1, Pallas kernels, local_step(): return tuple((o.reshape(-1) for o in copy_out(*outs)))  7.96 us

profile of v3, /device:TPU:0, one launch (start us, length us, event | category | flops | bytes accessed | tf_op | source)
XLA Modules:
  0.0 261.1 jit_solution(16065126739253884832)
XLA Ops:
  1.3 251.9 %adam_step.1 = (f32[2400,128]{1,0:T(8,128)S(1)}, f32[2400,128]{1,0:T(8,128)S(1)}, f32[2400,128]{1,0:T(8,128)S(1)}, f32[130,128]{1,0:T(8,128)S(1)}, f32[130,128]{...) custom-call(bf16[1,9830400]{1,0:T(2,128)(2,1)} %g.1, bf16[1,16640]{1,0:T(2,128)(2,1)} %gv.1, ...), custom_call_target="tpu_custom_call" | custom-call | tf_op jit(solution)/shard_map/adam_step/pallas_call | solution.py:526
  253.2 8.0 %copy_out.1 = (f32[2400,128]{1,0:T(8,128)}, f32[2400,128]{1,0:T(8,128)}, f32[2400,128]{1,0:T(8,128)}, f32[130,128]{1,0:T(8,128)}, f32[130,128]{1,0:T(8,128)}, /*...) custom-call(f32[2400,128]{1,0:T(8,128)S(1)} %get-tuple-element.21.refs_0_, ...), custom_call_target="tpu_custom_call" | custom-call | tf_op jit(solution)/shard_map/copy_out/pallas_call | solution.py:532

commit v4 on v3

--- a/solution.py
+++ b/solution.py
@@ -16,6 +16,10 @@
 BIAS_TWO = 1.0 - ADAM_BETA2 ** STEP
 
 DP = 32
+AG_CHUNKS = 15
+AG_ROWS = 160
+AG_AB = 32
+AG_CD = 48
 PIECE = 2400
 CHUNKS = 25
 ROWS = PIECE // CHUNKS
@@ -23,7 +27,7 @@
 RAB = 16
 RCD = HALF - RAB
 SKEW_RS = 2
-SKEW_AG = 2
+SKEW_AG = 1
 VEC = 130
 VPAD = 136
 MESH = pl.DeviceIdType.MESH
@@ -43,7 +47,7 @@
            stage, dense, pab, pcd, abz, er, cdr, abr, fr, gsum, ssq, clip, vs, vr, ns, nr,
            in_sem, pmv_sem, s0_send, s0_recv, rs_send, er_recv, cd_recv, ab_recv, f_recv,
            vec_send, vec_recv, norm_send, norm_recv,
-           ag_send, ag_ab, ag_cd, ag_cd1, ag_ab2, ag_ab3, ag_cd3, ag_d2d):
+           ag_send, ag_ab, ag_cd, ag_cd1, ag_h2, ag_h3, ag_d2d):
     me = lax.axis_index("dp")
     c = me % 2
     x = (me // 2) % 2
@@ -174,39 +178,46 @@
         def _():
             convert(k + 1)
 
-    def z_sends(k, t, bufs, recv, rsem):
-        @pl.when(z <= t)
-        def _():
-            dest = 3 + z - t
-            if t > 0:
-                @pl.when(nlow)
-                def _():
-                    wait(recv.at[k, t - 1], rsem.at[k, t - 1])
-                    bufs[k, dest] += recv[k, t - 1]
-            send(bufs.at[k, dest], recv.at[k, t], rs_send.at[k], rsem.at[k, t], up)
-
-        @pl.when(3 - z <= t)
-        def _():
-            dest = t - (3 - z)
-            if t > 0:
-                @pl.when(nhigh)
-                def _():
-                    old = 0 if t == 1 else t + 1
-                    wait(recv.at[k, old], rsem.at[k, old])
-                    bufs[k, dest] += recv[k, old]
-            new = 0 if t == 0 else t + 2
-            send(bufs.at[k, dest], recv.at[k, new], rs_send.at[k], rsem.at[k, new], down)
+    def z_first(k, bufs, recv, rsem):
+        @pl.when(z == 0)
+        def _():
+            send(bufs.at[k, pl.ds(1, 3)], recv.at[k, pl.ds(0, 3)], rs_send.at[k], rsem.at[k, 0], up)
+
+        @pl.when(z == 3)
+        def _():
+            send(bufs.at[k, pl.ds(0, 3)], recv.at[k, pl.ds(0, 3)], rs_send.at[k], rsem.at[k, 0], down)
+
+    def z_second(k, bufs, recv, rsem):
+        @pl.when(z == 1)
+        def _():
+            wait(recv.at[k, pl.ds(0, 3)], rsem.at[k, 0])
+            bufs[k, 1:4] += recv[k, 0:3]
+            send(bufs.at[k, pl.ds(2, 2)], recv.at[k, pl.ds(3, 2)], rs_send.at[k], rsem.at[k, 1], up)
+
+        @pl.when(z == 2)
+        def _():
+            wait(recv.at[k, pl.ds(0, 3)], rsem.at[k, 0])
+            bufs[k, 0:3] += recv[k, 0:3]
+            send(bufs.at[k, pl.ds(0, 2)], recv.at[k, pl.ds(3, 2)], rs_send.at[k], rsem.at[k, 1], down)
+
+    def z_third(k, bufs, recv, rsem):
+        @pl.when(z == 1)
+        def _():
+            wait(recv.at[k, pl.ds(3, 2)], rsem.at[k, 1])
+            bufs[k, 0:2] += recv[k, 3:5]
+            send(bufs.at[k, 0], recv.at[k, 0], rs_send.at[k], rsem.at[k, 0], down)
+
+        @pl.when(z == 2)
+        def _():
+            wait(recv.at[k, pl.ds(3, 2)], rsem.at[k, 1])
+            bufs[k, 2:4] += recv[k, 3:5]
+            send(bufs.at[k, 3], recv.at[k, 0], rs_send.at[k], rsem.at[k, 0], up)
 
     def z_final(k, bufs, recv, rsem):
-        @pl.when(nlow)
-        def _():
-            wait(recv.at[k, 2], rsem.at[k, 2])
-            bufs[k, z] += recv[k, 2]
-
-        @pl.when(nhigh)
-        def _():
-            wait(recv.at[k, 4], rsem.at[k, 4])
-            bufs[k, z] += recv[k, 4]
+        @pl.when(jnp.logical_not(mid))
+        def _():
+            wait(recv.at[k, 0], rsem.at[k, 0])
+            bufs[k, z] += recv[k, 0]
 
     def stage1(k):
         dslot = k % 4
@@ -224,25 +235,25 @@
             lax.fori_loop(0, 8, add, 0)
         send(pab.at[k, 0, 1 - y], er.at[k, 0], rs_send.at[k], er_recv.at[k], ys)
         send(pab.at[k, 1, 1 - x], er.at[k, 1], rs_send.at[k], er_recv.at[k], xs)
-        z_sends(k, 0, pcd, cdr, cd_recv)
+        z_first(k, pcd, cdr, cd_recv)
 
     def stage2(k):
-        z_sends(k, 1, pcd, cdr, cd_recv)
+        z_second(k, pcd, cdr, cd_recv)
         wait(er.at[k], er_recv.at[k])
         for zz in range(4):
             abz[k, zz, 0] = pab[k, 0, y, zz] + er[k, 0, zz]
             abz[k, zz, 1] = pab[k, 1, x, zz] + er[k, 1, zz]
-        z_sends(k, 0, abz, abr, ab_recv)
+        z_first(k, abz, abr, ab_recv)
 
     def stage3(k):
-        z_sends(k, 2, pcd, cdr, cd_recv)
-        z_sends(k, 1, abz, abr, ab_recv)
+        z_third(k, pcd, cdr, cd_recv)
+        z_second(k, abz, abr, ab_recv)
 
     def stage4(k):
         z_final(k, pcd, cdr, cd_recv)
         send(pcd.at[k, z, 0, 1 - y], fr.at[k, 0], rs_send.at[k], f_recv.at[k], ys)
         send(pcd.at[k, z, 1, 1 - x], fr.at[k, 1], rs_send.at[k], f_recv.at[k], xs)
-        z_sends(k, 2, abz, abr, ab_recv)
+        z_third(k, abz, abr, ab_recv)
 
     def stage5(k):
         z_final(k, abz, abr, ab_recv)
@@ -296,8 +307,11 @@
     wait(mo, pmv_sem.at[1])
     wait(vo, pmv_sem.at[2])
 
-    def ag_rows(k, off, num):
-        return pl.ds(pl.multiple_of(k * ROWS + off, 16), num)
+    def cut(k, off, num):
+        return pl.ds(pl.multiple_of(k * AG_ROWS + off, 16), num)
+
+    def rows_of(k):
+        return (cut(k, 0, AG_AB), cut(k, AG_AB, AG_AB), cut(k, 2 * AG_AB, AG_CD), cut(k, 2 * AG_AB + AG_CD, AG_CD))
 
     full = slice(None)
 
@@ -307,150 +321,141 @@
     def push(ref, k, rsem, to):
         send(ref, ref, ag_send.at[k], rsem, to)
 
+    def sides(dist, fn):
+        if dist == 0:
+            fn(z, None)
+            return
+
+        @pl.when(z - dist >= 0)
+        def _():
+            fn(z - dist, 0)
+
+        @pl.when(z + dist <= 3)
+        def _():
+            fn(z + dist, 1)
+
+    def along_z(fn):
+        @pl.when(nhigh)
+        def _():
+            fn(0, up)
+
+        @pl.when(nlow)
+        def _():
+            fn(1, down)
+
+    def onward_z(side, dist, fn):
+        if dist == 0:
+            along_z(fn)
+        elif dist < 3 and side == 0:
+            @pl.when(nhigh)
+            def _():
+                fn(0, up)
+        elif dist < 3:
+            @pl.when(nlow)
+            def _():
+                fn(1, down)
+
+    def ab_arrived(k, dist):
+        ra, rb = rows_of(k)[:2]
+        ab = cut(k, 0, 2 * AG_AB)
+
+        def fn(zz, side):
+            if dist:
+                wait(region(0, 0, 0, ab), ag_ab.at[k, side, dist - 1])
+            onward_z(side, dist, lambda way, to: push(region(zz, y, x, ab), k, ag_ab.at[k, way, dist], to))
+            push(region(zz, y, x, ra), k, ag_h2.at[k, zz], ys)
+            push(region(zz, y, x, rb), k, ag_h2.at[k, zz], xs)
+
+        sides(dist, fn)
+
+    def ab_second(k, dist):
+        ra, rb = rows_of(k)[:2]
+
+        def fn(zz, side):
+            wait(region(0, 0, 0, cut(k, 0, 2 * AG_AB)), ag_h2.at[k, zz])
+            push(region(zz, full, x, ra), k, ag_h3.at[k], xs)
+            push(region(zz, y, full, rb), k, ag_h3.at[k], ys)
+
+        sides(dist, fn)
+
+    def cd_arrived(k, dist):
+        rc, rd = rows_of(k)[2:]
+
+        def fn(zz, side):
+            if dist == 0:
+                wait(region(0, 0, 0, cut(k, 0, 2 * AG_CD)), ag_cd1.at[k])
+            else:
+                wait(pb.at[0, 0, full, full, rc], ag_cd.at[k, side, dist - 1])
+
+            def on(way, to):
+                push(region(zz, full, x, rc), k, ag_cd.at[k, way, dist], to)
+                push(region(zz, y, full, rd), k, ag_cd.at[k, way, dist], to)
+
+            onward_z(side, dist, on)
+            push(region(zz, full, x, rc), k, ag_h3.at[k], xs)
+            push(region(zz, y, full, rd), k, ag_h3.at[k], ys)
+
+        sides(dist, fn)
+
     def ag0(k):
         def upd(b, carry):
-            rows = pl.ds(pl.multiple_of(k * ROWS + b * 32, 16), 32)
+            rows = pl.ds(pl.multiple_of(k * AG_ROWS + b * 32, 16), 32)
             new = adam_update(gsum[rows] * clip[0:1], po[rows], mo[rows], vo[rows], rate, WEIGHT_DECAY)
             po[rows], mo[rows], vo[rows] = new
             pb[z, y, x, c, rows] = new[0].astype(BF16)
             return carry
-        lax.fori_loop(0, ROWS // 32, upd, 0)
-        ab = ag_rows(k, 0, 2 * RAB)
-
-        @pl.when(nhigh)
-        def _():
-            push(region(z, y, x, ab), k, ag_ab.at[k, 0, 0], up)
-
-        @pl.when(nlow)
-        def _():
-            push(region(z, y, x, ab), k, ag_ab.at[k, 1, 0], down)
-
-        push(region(z, y, x, ag_rows(k, 2 * RAB, RCD)), k, ag_cd1.at[k], ys)
-        push(region(z, y, x, ag_rows(k, 2 * RAB + RCD, RCD)), k, ag_cd1.at[k], xs)
-
-    def z_ab(k, t):
-        ab = ag_rows(k, 0, 2 * RAB)
-        one = region(0, 0, 0, ab)
-
-        @pl.when(z - 1 - t >= 0)
-        def _():
-            wait(one, ag_ab.at[k, 0, t])
-            if t < 2:
-                @pl.when(nhigh)
-                def _():
-                    push(region(z - 1 - t, y, x, ab), k, ag_ab.at[k, 0, t + 1], up)
-
-        @pl.when(z + 1 + t <= 3)
-        def _():
-            wait(one, ag_ab.at[k, 1, t])
-            if t < 2:
-                @pl.when(nlow)
-                def _():
-                    push(region(z + 1 + t, y, x, ab), k, ag_ab.at[k, 1, t + 1], down)
-
-    def cd_push(k, zz, d, t, to):
-        push(region(zz, full, x, ag_rows(k, 2 * RAB, RCD)), k, ag_cd.at[k, d, t], to)
-        push(region(zz, y, full, ag_rows(k, 2 * RAB + RCD, RCD)), k, ag_cd.at[k, d, t], to)
-
-    def z_cd(k, t):
-        both = pb.at[0, 0, full, full, ag_rows(k, 2 * RAB, RCD)]
-
-        @pl.when(z - 1 - t >= 0)
-        def _():
-            wait(both, ag_cd.at[k, 0, t])
-            if t < 2:
-                @pl.when(nhigh)
-                def _():
-                    cd_push(k, z - 1 - t, 0, t + 1, up)
-
-        @pl.when(z + 1 + t <= 3)
-        def _():
-            wait(both, ag_cd.at[k, 1, t])
-            if t < 2:
-                @pl.when(nlow)
-                def _():
-                    cd_push(k, z + 1 + t, 1, t + 1, down)
-
-    def ag1(k):
-        wait(pb.at[0, 0, 0, full, ag_rows(k, 2 * RAB, RCD)], ag_cd1.at[k])
-
-        @pl.when(nhigh)
-        def _():
-            cd_push(k, z, 0, 0, up)
-
-        @pl.when(nlow)
-        def _():
-            cd_push(k, z, 1, 0, down)
-
-        z_ab(k, 0)
-
-    def ag2(k):
-        z_ab(k, 1)
-        z_cd(k, 0)
-
-    def ag3(k):
-        z_ab(k, 2)
-        ra = ag_rows(k, 0, RAB)
-        rb = ag_rows(k, RAB, RAB)
-        push(region(full, y, x, ra), k, ag_ab2.at[k], ys)
-        push(region(full, y, x, rb), k, ag_ab2.at[k], xs)
-        push(region(full, y, x, ag_rows(k, 0, 2 * RAB)), k, ag_d2d.at[k], partner)
-        z_cd(k, 1)
-
-    def ag4(k):
-        ra = ag_rows(k, 0, RAB)
-        rb = ag_rows(k, RAB, RAB)
-        rc = ag_rows(k, 2 * RAB, RCD)
-        rd = ag_rows(k, 2 * RAB + RCD, RCD)
-        wait(pb.at[0, 0, full, full, ag_rows(k, 0, 2 * RAB)], ag_ab2.at[k])
-        push(region(full, full, x, ra), k, ag_ab3.at[k], xs)
-        push(region(full, y, full, rb), k, ag_ab3.at[k], ys)
-        push(region(full, 1 - y, x, ra), k, ag_d2d.at[k], partner)
-        push(region(full, y, 1 - x, rb), k, ag_d2d.at[k], partner)
-        z_cd(k, 2)
-        push(region(full, full, x, rc), k, ag_cd3.at[k], xs)
-        push(region(full, y, full, rd), k, ag_cd3.at[k], ys)
-        push(region(full, full, x, rc), k, ag_d2d.at[k], partner)
-        push(region(full, y, full, rd), k, ag_d2d.at[k], partner)
+        lax.fori_loop(0, AG_ROWS // 32, upd, 0)
+        rc, rd = rows_of(k)[2:]
+        push(region(z, y, x, rc), k, ag_cd1.at[k], ys)
+        push(region(z, y, x, rd), k, ag_cd1.at[k], xs)
+        ab_arrived(k, 0)
+
+    def middle(s):
+        def fn(k):
+            cd_arrived(k, s - 1)
+            if s <= 3:
+                ab_arrived(k, s)
+            ab_second(k, s - 1)
+        return fn
 
     def ag5(k):
-        wait(pb.at[0, full, full, full, ag_rows(k, 0, 2 * RAB)], ag_ab3.at[k])
-        push(region(full, full, 1 - x, ag_rows(k, 0, RAB)), k, ag_d2d.at[k], partner)
-        push(region(full, 1 - y, full, ag_rows(k, RAB, RAB)), k, ag_d2d.at[k], partner)
-        wait(pb.at[full, full, full, 0, ag_rows(k, 2 * RAB, RCD)], ag_cd3.at[k])
-        push(region(full, full, 1 - x, ag_rows(k, 2 * RAB, RCD)), k, ag_d2d.at[k], partner)
-        push(region(full, 1 - y, full, ag_rows(k, 2 * RAB + RCD, RCD)), k, ag_d2d.at[k], partner)
+        wait(pb.at[0, full, full, full, cut(k, 0, AG_ROWS)], ag_h3.at[k])
+        push(region(full, full, full, cut(k, 0, AG_ROWS)), k, ag_d2d.at[k], partner)
 
     def ag_iter(i, carry):
-        for s, fn in enumerate((ag0, ag1, ag2, ag3, ag4, ag5)):
+        for s, fn in enumerate((ag0, middle(1), middle(2), middle(3), middle(4), ag5)):
             k = i - SKEW_AG * s
 
-            @pl.when((k >= 0) & (k < CHUNKS))
+            @pl.when((k >= 0) & (k < AG_CHUNKS))
             def _(fn=fn, k=k):
                 fn(k)
         return carry
 
-    lax.fori_loop(0, CHUNKS + 5 * SKEW_AG, ag_iter, 0)
+    lax.fori_loop(0, AG_CHUNKS + 5 * SKEW_AG, ag_iter, 0)
 
     newv = adam_update(gvec * clip[0:1], pv[...], mv[...], vv[...], rate, 0.0)
     pvo[...], mvo[...], vvo[...] = newv
 
-    def drain(k, carry):
-        wait(pb.at[full, full, full, 0, ag_rows(k, 0, ROWS)], ag_d2d.at[k])
-        base, along = 24 * RAB + 18 * RCD + 16 * ROWS, 2 * RAB + 4 * RCD
-
-        @pl.when(mid)
-        def _():
-            wait(pb.at[0, 0, full, full, pl.ds(0, (base + 5 * along) // 4)], ag_send.at[k])
-
-        @pl.when(jnp.logical_not(mid))
-        def _():
-            wait(pb.at[0, 0, 0, full, pl.ds(0, (base + along) // 2)], ag_send.at[k])
-
+    def drain_rs(k, carry):
         wait(gsum.at[pl.ds(0, 14 * HALF)], rs_send.at[k])
         return carry
 
-    lax.fori_loop(0, CHUNKS, drain, 0)
+    def drain_ag(k, carry):
+        wait(pb.at[full, full, full, 0, cut(k, 0, AG_ROWS)], ag_d2d.at[k])
+        base, along = 24 * AG_AB + 18 * AG_CD + 16 * AG_ROWS, 2 * AG_AB + 4 * AG_CD
+
+        @pl.when(mid)
+        def _():
+            wait(pb.at[0, 0, full, full, pl.ds(0, (base + 5 * along) // 4)], ag_send.at[k])
+
+        @pl.when(jnp.logical_not(mid))
+        def _():
+            wait(pb.at[0, 0, 0, full, pl.ds(0, (base + along) // 2)], ag_send.at[k])
+
+        return carry
+
+    lax.fori_loop(0, CHUNKS, drain_rs, 0)
+    lax.fori_loop(0, AG_CHUNKS, drain_ag, 0)
     for s in range(4):
         wait(dense.at[s, :, pl.ds(1, 3)], s0_send.at[s])
     for j in range(5):
@@ -473,7 +478,7 @@
     vm = pl.BlockSpec(memory_space=pltpu.VMEM)
     hbm = pl.BlockSpec(memory_space=pl.ANY)
     dma = pltpu.SemaphoreType.DMA
-    K = CHUNKS
+    K, G = CHUNKS, AG_CHUNKS
 
     call = pl.pallas_call(
         kernel,
@@ -502,9 +507,9 @@
             pltpu.VMEM((5, VPAD, 128), F32),
             pltpu.VMEM((1, 128), F32),
             pltpu.VMEM((DP, 1, 128), F32),
-            dma((2,)), dma((3,)), dma((4,)), dma((K,)), dma((K,)), dma((K,)), dma((K, 5)), dma((K, 5)), dma((K,)),
+            dma((2,)), dma((3,)), dma((4,)), dma((K,)), dma((K,)), dma((K,)), dma((K, 2)), dma((K, 2)), dma((K,)),
             dma((5,)), dma((5,)), dma, dma,
-            dma((K,)), dma((K, 2, 3)), dma((K, 2, 3)), dma((K,)), dma((K,)), dma((K,)), dma((K,)), dma((K,)),
+            dma((G,)), dma((G, 2, 3)), dma((G, 2, 3)), dma((G,)), dma((G, 4)), dma((G,)), dma((G,)),
         ],
         compiler_params=pltpu.CompilerParams(
             collective_id=0, has_side_effects=True, vmem_limit_bytes=37 * 2 ** 20

time: 261 us -> 251 us (0.962)
  Pallas kernels: 260 us -> 250 us
    pallas_call x1, Pallas kernels: 252 us -> 242 us  [local_step(): call(g_mat, g_vec, p_mat.reshape(PIECE, 128), m_mat.reshape(PIECE, 128),...]
where the time goes in v4:
time: 251 us
  Pallas kernels  250 us (100%)
    pallas_call x1, Pallas kernels, local_step(): call(g_mat, g_vec, p_mat.reshape(PIECE, 128), m_mat.reshape(PIECE, 128),...  242 us
    pallas_call x1, Pallas kernels, local_step(): return tuple((o.reshape(-1) for o in copy_out(*outs)))  7.96 us

profile of v4, /device:TPU:0, one launch (start us, length us, event | category | flops | bytes accessed | tf_op | source)
XLA Modules:
  0.0 251.1 jit_solution(1588963535192666913)
XLA Ops:
  1.3 241.9 %adam_step.1 = (f32[2400,128]{1,0:T(8,128)S(1)}, f32[2400,128]{1,0:T(8,128)S(1)}, f32[2400,128]{1,0:T(8,128)S(1)}, f32[130,128]{1,0:T(8,128)S(1)}, f32[130,128]{...) custom-call(bf16[1,9830400]{1,0:T(2,128)(2,1)} %g.1, bf16[1,16640]{1,0:T(2,128)(2,1)} %gv.1, ...), custom_call_target="tpu_custom_call" | custom-call | tf_op jit(solution)/shard_map/adam_step/pallas_call | solution.py:531
  243.2 8.0 %copy_out.1 = (f32[2400,128]{1,0:T(8,128)}, f32[2400,128]{1,0:T(8,128)}, f32[2400,128]{1,0:T(8,128)}, f32[130,128]{1,0:T(8,128)}, f32[130,128]{1,0:T(8,128)}, /*...) custom-call(f32[2400,128]{1,0:T(8,128)S(1)} %get-tuple-element.21.refs_0_, ...), custom_call_target="tpu_custom_call" | custom-call | tf_op jit(solution)/shard_map/copy_out/pallas_call | solution.py:537

commit v5 on v4

--- a/solution.py
+++ b/solution.py
@@ -18,8 +18,8 @@
 DP = 32
 AG_CHUNKS = 15
 AG_ROWS = 160
-AG_AB = 32
-AG_CD = 48
+AG_AB = 16
+AG_CD = 64
 PIECE = 2400
 CHUNKS = 25
 ROWS = PIECE // CHUNKS
@@ -181,43 +181,43 @@
     def z_first(k, bufs, recv, rsem):
         @pl.when(z == 0)
         def _():
-            send(bufs.at[k, pl.ds(1, 3)], recv.at[k, pl.ds(0, 3)], rs_send.at[k], rsem.at[k, 0], up)
+            send(bufs.at[pl.ds(1, 3)], recv.at[pl.ds(0, 3)], rs_send.at[k], rsem.at[0], up)
 
         @pl.when(z == 3)
         def _():
-            send(bufs.at[k, pl.ds(0, 3)], recv.at[k, pl.ds(0, 3)], rs_send.at[k], rsem.at[k, 0], down)
+            send(bufs.at[pl.ds(0, 3)], recv.at[pl.ds(0, 3)], rs_send.at[k], rsem.at[0], down)
 
     def z_second(k, bufs, recv, rsem):
         @pl.when(z == 1)
         def _():
-            wait(recv.at[k, pl.ds(0, 3)], rsem.at[k, 0])
-            bufs[k, 1:4] += recv[k, 0:3]
-            send(bufs.at[k, pl.ds(2, 2)], recv.at[k, pl.ds(3, 2)], rs_send.at[k], rsem.at[k, 1], up)
+            wait(recv.at[pl.ds(0, 3)], rsem.at[0])
+            bufs[1:4] += recv[0:3]
+            send(bufs.at[pl.ds(2, 2)], recv.at[pl.ds(3, 2)], rs_send.at[k], rsem.at[1], up)
 
         @pl.when(z == 2)
         def _():
-            wait(recv.at[k, pl.ds(0, 3)], rsem.at[k, 0])
-            bufs[k, 0:3] += recv[k, 0:3]
-            send(bufs.at[k, pl.ds(0, 2)], recv.at[k, pl.ds(3, 2)], rs_send.at[k], rsem.at[k, 1], down)
+            wait(recv.at[pl.ds(0, 3)], rsem.at[0])
+            bufs[0:3] += recv[0:3]
+            send(bufs.at[pl.ds(0, 2)], recv.at[pl.ds(3, 2)], rs_send.at[k], rsem.at[1], down)
 
     def z_third(k, bufs, recv, rsem):
         @pl.when(z == 1)
         def _():
-            wait(recv.at[k, pl.ds(3, 2)], rsem.at[k, 1])
-            bufs[k, 0:2] += recv[k, 3:5]
-            send(bufs.at[k, 0], recv.at[k, 0], rs_send.at[k], rsem.at[k, 0], down)
+            wait(recv.at[pl.ds(3, 2)], rsem.at[1])
+            bufs[0:2] += recv[3:5]
+            send(bufs.at[0], recv.at[0], rs_send.at[k], rsem.at[0], down)
 
         @pl.when(z == 2)
         def _():
-            wait(recv.at[k, pl.ds(3, 2)], rsem.at[k, 1])
-            bufs[k, 2:4] += recv[k, 3:5]
-            send(bufs.at[k, 3], recv.at[k, 0], rs_send.at[k], rsem.at[k, 0], up)
+            wait(recv.at[pl.ds(3, 2)], rsem.at[1])
+            bufs[2:4] += recv[3:5]
+            send(bufs.at[3], recv.at[0], rs_send.at[k], rsem.at[0], up)
 
     def z_final(k, bufs, recv, rsem):
         @pl.when(jnp.logical_not(mid))
         def _():
-            wait(recv.at[k, 0], rsem.at[k, 0])
-            bufs[k, z] += recv[k, 0]
+            wait(recv.at[0], rsem.at[0])
+            bufs[z] += recv[0]
 
     def stage1(k):
         dslot = k % 4
@@ -230,40 +230,44 @@
                     off = pl.multiple_of(roff(k, d) + j * 8 * HALF + b * HALF, 16)
                     tot = tot + pb[(*rpiece(k, d), pl.ds(off, HALF))].astype(F32)
                 pab[k, d, b % 2, b // 2] = tot[0:RAB]
-                pcd[k, b // 2, d, b % 2] = tot[RAB:HALF]
+                pcd[k, d, b // 2, b % 2] = tot[RAB:HALF]
                 return carry
             lax.fori_loop(0, 8, add, 0)
         send(pab.at[k, 0, 1 - y], er.at[k, 0], rs_send.at[k], er_recv.at[k], ys)
         send(pab.at[k, 1, 1 - x], er.at[k, 1], rs_send.at[k], er_recv.at[k], xs)
-        z_first(k, pcd, cdr, cd_recv)
+        for d in range(2):
+            z_first(k, pcd.at[k, d], cdr.at[k, d], cd_recv.at[k, d])
 
     def stage2(k):
-        z_second(k, pcd, cdr, cd_recv)
+        for d in range(2):
+            z_second(k, pcd.at[k, d], cdr.at[k, d], cd_recv.at[k, d])
         wait(er.at[k], er_recv.at[k])
         for zz in range(4):
             abz[k, zz, 0] = pab[k, 0, y, zz] + er[k, 0, zz]
             abz[k, zz, 1] = pab[k, 1, x, zz] + er[k, 1, zz]
-        z_first(k, abz, abr, ab_recv)
+        z_first(k, abz.at[k], abr.at[k], ab_recv.at[k])
 
     def stage3(k):
-        z_third(k, pcd, cdr, cd_recv)
-        z_second(k, abz, abr, ab_recv)
+        for d in range(2):
+            z_third(k, pcd.at[k, d], cdr.at[k, d], cd_recv.at[k, d])
+        z_second(k, abz.at[k], abr.at[k], ab_recv.at[k])
 
     def stage4(k):
-        z_final(k, pcd, cdr, cd_recv)
-        send(pcd.at[k, z, 0, 1 - y], fr.at[k, 0], rs_send.at[k], f_recv.at[k], ys)
-        send(pcd.at[k, z, 1, 1 - x], fr.at[k, 1], rs_send.at[k], f_recv.at[k], xs)
-        z_third(k, abz, abr, ab_recv)
+        for d in range(2):
+            z_final(k, pcd.at[k, d], cdr.at[k, d], cd_recv.at[k, d])
+        send(pcd.at[k, 0, z, 1 - y], fr.at[k, 0], rs_send.at[k], f_recv.at[k], ys)
+        send(pcd.at[k, 1, z, 1 - x], fr.at[k, 1], rs_send.at[k], f_recv.at[k], xs)
+        z_third(k, abz.at[k], abr.at[k], ab_recv.at[k])
 
     def stage5(k):
-        z_final(k, abz, abr, ab_recv)
+        z_final(k, abz.at[k], abr.at[k], ab_recv.at[k])
         wait(fr.at[k], f_recv.at[k])
         base = pl.multiple_of(k * ROWS, 16)
         parts = (
             (0, RAB, abz[k, z, 0]),
-            (RAB, RCD, pcd[k, z, 0, y] + fr[k, 0]),
+            (RAB, RCD, pcd[k, 0, z, y] + fr[k, 0]),
             (HALF, RAB, abz[k, z, 1]),
-            (HALF + RAB, RCD, pcd[k, z, 1, x] + fr[k, 1]),
+            (HALF + RAB, RCD, pcd[k, 1, z, x] + fr[k, 1]),
         )
         acc = ssq[...]
         for off, num, val in parts:
@@ -494,10 +498,10 @@
             pltpu.VMEM((2, DP, 1, ROWS * 128), BF16),
             pltpu.VMEM((4, 2, 4, 8 * HALF, 128), BF16),
             pltpu.VMEM((K, 2, 2, 4, RAB, 128), F32),
-            pltpu.VMEM((K, 4, 2, 2, RCD, 128), F32),
+            pltpu.VMEM((K, 2, 4, 2, RCD, 128), F32),
             pltpu.VMEM((K, 4, 2, RAB, 128), F32),
             pltpu.VMEM((K, 2, 4, RAB, 128), F32),
-            pltpu.VMEM((K, 5, 2, 2, RCD, 128), F32),
+            pltpu.VMEM((K, 2, 5, 2, RCD, 128), F32),
             pltpu.VMEM((K, 5, 2, RAB, 128), F32),
             pltpu.VMEM((K, 2, RCD, 128), F32),
             pltpu.VMEM((PIECE, 128), F32),
@@ -507,7 +511,7 @@
             pltpu.VMEM((5, VPAD, 128), F32),
             pltpu.VMEM((1, 128), F32),
             pltpu.VMEM((DP, 1, 128), F32),
-            dma((2,)), dma((3,)), dma((4,)), dma((K,)), dma((K,)), dma((K,)), dma((K, 2)), dma((K, 2)), dma((K,)),
+            dma((2,)), dma((3,)), dma((4,)), dma((K,)), dma((K,)), dma((K,)), dma((K, 2, 2)), dma((K, 2)), dma((K,)),
             dma((5,)), dma((5,)), dma, dma,
             dma((G,)), dma((G, 2, 3)), dma((G, 2, 3)), dma((G,)), dma((G, 4)), dma((G,)), dma((G,)),
         ],

time: 251 us -> 257 us (1.024)
  Pallas kernels: 250 us -> 255 us
    pallas_call x1, Pallas kernels: 242 us -> 247 us  [local_step(): call(g_mat, g_vec, p_mat.reshape(PIECE, 128), m_mat.reshape(PIECE, 128),...]
where the time goes in v5:
time: 257 us
  Pallas kernels  255 us (99%)
    pallas_call x1, Pallas kernels, local_step(): call(g_mat, g_vec, p_mat.reshape(PIECE, 128), m_mat.reshape(PIECE, 128),...  247 us
    pallas_call x1, Pallas kernels, local_step(): return tuple((o.reshape(-1) for o in copy_out(*outs)))  7.96 us

profile of v5, /device:TPU:0, one launch (start us, length us, event | category | flops | bytes accessed | tf_op | source)
XLA Modules:
  0.0 256.5 jit_solution(6529079829283905278)
XLA Ops:
  1.3 247.3 %adam_step.1 = (f32[2400,128]{1,0:T(8,128)S(1)}, f32[2400,128]{1,0:T(8,128)S(1)}, f32[2400,128]{1,0:T(8,128)S(1)}, f32[130,128]{1,0:T(8,128)S(1)}, f32[130,128]{...) custom-call(bf16[1,9830400]{1,0:T(2,128)(2,1)} %g.1, bf16[1,16640]{1,0:T(2,128)(2,1)} %gv.1, ...), custom_call_target="tpu_custom_call" | custom-call | tf_op jit(solution)/shard_map/adam_step/pallas_call | solution.py:535
  248.6 8.0 %copy_out.1 = (f32[2400,128]{1,0:T(8,128)}, f32[2400,128]{1,0:T(8,128)}, f32[2400,128]{1,0:T(8,128)}, f32[130,128]{1,0:T(8,128)}, f32[130,128]{1,0:T(8,128)}, /*...) custom-call(f32[2400,128]{1,0:T(8,128)S(1)} %get-tuple-element.21.refs_0_, ...), custom_call_target="tpu_custom_call" | custom-call | tf_op jit(solution)/shard_map/copy_out/pallas_call | solution.py:541

commit v6 on v5

--- a/solution.py
+++ b/solution.py
@@ -18,13 +18,13 @@
 DP = 32
 AG_CHUNKS = 15
 AG_ROWS = 160
-AG_AB = 16
-AG_CD = 64
+AG_AB = 40
+AG_CD = 40
 PIECE = 2400
 CHUNKS = 25
 ROWS = PIECE // CHUNKS
 HALF = ROWS // 2
-RAB = 16
+RAB = 24
 RCD = HALF - RAB
 SKEW_RS = 2
 SKEW_AG = 1
@@ -312,7 +312,7 @@
     wait(vo, pmv_sem.at[2])
 
     def cut(k, off, num):
-        return pl.ds(pl.multiple_of(k * AG_ROWS + off, 16), num)
+        return pl.ds(pl.multiple_of(k * AG_ROWS + off, 8), num)
 
     def rows_of(k):
         return (cut(k, 0, AG_AB), cut(k, AG_AB, AG_AB), cut(k, 2 * AG_AB, AG_CD), cut(k, 2 * AG_AB + AG_CD, AG_CD))

time: 257 us -> 255 us (level)
  no operation moved by 1% of the time
where the time goes in v6:
time: 255 us
  Pallas kernels  254 us (100%)
    pallas_call x1, Pallas kernels, local_step(): call(g_mat, g_vec, p_mat.reshape(PIECE, 128), m_mat.reshape(PIECE, 128),...  246 us
    pallas_call x1, Pallas kernels, local_step(): return tuple((o.reshape(-1) for o in copy_out(*outs)))  7.96 us

profile of v6, /device:TPU:0, one launch (start us, length us, event | category | flops | bytes accessed | tf_op | source)
XLA Modules:
  0.0 255.1 jit_solution(17072269532823021067)
XLA Ops:
  1.3 245.8 %adam_step.1 = (f32[2400,128]{1,0:T(8,128)S(1)}, f32[2400,128]{1,0:T(8,128)S(1)}, f32[2400,128]{1,0:T(8,128)S(1)}, f32[130,128]{1,0:T(8,128)S(1)}, f32[130,128]{...) custom-call(bf16[1,9830400]{1,0:T(2,128)(2,1)} %g.1, bf16[1,16640]{1,0:T(2,128)(2,1)} %gv.1, ...), custom_call_target="tpu_custom_call" | custom-call | tf_op jit(solution)/shard_map/adam_step/pallas_call | solution.py:535
  247.1 8.0 %copy_out.1 = (f32[2400,128]{1,0:T(8,128)}, f32[2400,128]{1,0:T(8,128)}, f32[2400,128]{1,0:T(8,128)}, f32[130,128]{1,0:T(8,128)}, f32[130,128]{1,0:T(8,128)}, /*...) custom-call(f32[2400,128]{1,0:T(8,128)S(1)} %get-tuple-element.21.refs_0_, ...), custom_call_target="tpu_custom_call" | custom-call | tf_op jit(solution)/shard_map/copy_out/pallas_call | solution.py:541

commit v7 on v6

--- a/solution.py
+++ b/solution.py
@@ -16,18 +16,19 @@
 BIAS_TWO = 1.0 - ADAM_BETA2 ** STEP
 
 DP = 32
-AG_CHUNKS = 15
-AG_ROWS = 160
-AG_AB = 40
-AG_CD = 40
+AG_CHUNKS = 10
+AG_ROWS = 240
+AG_AB = 48
+AG_CD = 72
 PIECE = 2400
-CHUNKS = 25
+CHUNKS = 50
 ROWS = PIECE // CHUNKS
 HALF = ROWS // 2
-RAB = 24
+RAB = 8
 RCD = HALF - RAB
 SKEW_RS = 2
-SKEW_AG = 1
+AG_STAGES = (0, 2, 3, 4, 5, 6)
+SLOTS = 16
 VEC = 130
 VPAD = 136
 MESH = pl.DeviceIdType.MESH
@@ -44,7 +45,7 @@
 
 def kernel(g, gv, p, m, v, pv, mv, vv, lr,
            po, mo, vo, pvo, mvo, vvo, pb,
-           stage, dense, pab, pcd, abz, er, cdr, abr, fr, gsum, ssq, clip, vs, vr, ns, nr,
+           gvb, stage, dense, pab, pcd, abz, er, cdr, abr, fr, gsum, ssq, clip, vs, vr, ns, nr,
            in_sem, pmv_sem, s0_send, s0_recv, rs_send, er_recv, cd_recv, ab_recv, f_recv,
            vec_send, vec_recv, norm_send, norm_recv,
            ag_send, ag_ab, ag_cd, ag_cd1, ag_h2, ag_h3, ag_d2d):
@@ -85,9 +86,6 @@
         lax.fori_loop(0, DP, one, 0)
 
     fetch(0, 0)
-    pltpu.make_async_copy(p, po, pmv_sem.at[0]).start()
-    pltpu.make_async_copy(m, mo, pmv_sem.at[1]).start()
-    pltpu.make_async_copy(v, vo, pmv_sem.at[2]).start()
 
     barrier = pltpu.get_barrier_semaphore()
     for nb in (partner, xs, xo, ys, yo, z2):
@@ -101,9 +99,6 @@
     def _():
         pl.semaphore_signal(barrier, inc=1, device_id=(down,), device_id_type=MESH)
 
-    vs[0, 0:128] = gv[0:1, 0:16384].astype(F32).reshape(128, 128)
-    vs[0, 128:VPAD] = jnp.zeros((VPAD - 128, 128), F32)
-    vs[0, 128:VEC] = gv[0:1, 16384:16640].astype(F32).reshape(2, 128)
     ssq[...] = jnp.zeros((8, 128), F32)
 
     mid = (z >= 1) & (z <= 2)
@@ -119,8 +114,17 @@
 
     partners = (partner, xs, ys, z1, z2)
 
+    loads = ((gv, gvb), (p, po), (m, mo), (v, vo), (pv, pvo), (mv, mvo), (vv, vvo))
+
     def vec_step(j):
-        if j > 0:
+        if j == 0:
+            for i, (src, dst) in enumerate(loads):
+                pltpu.make_async_copy(src, dst, pmv_sem.at[i]).start()
+            wait(gvb, pmv_sem.at[0])
+            vs[0, 0:128] = gvb[0:1, 0:16384].astype(F32).reshape(128, 128)
+            vs[0, 128:VPAD] = jnp.zeros((VPAD - 128, 128), F32)
+            vs[0, 128:VEC] = gvb[0:1, 16384:16640].astype(F32).reshape(2, 128)
+        else:
             wait(vr.at[j - 1], vec_recv.at[j - 1])
             vs[j] = vs[j - 1] + vr[j - 1]
         if j < 5:
@@ -153,26 +157,29 @@
         wait(stage.at[slot], in_sem.at[slot])
 
         def conv(b, carry):
-            row = pl.multiple_of(b * HALF, 16)
+            row = pl.multiple_of(b * 2 * HALF, 16)
             for d in range(2):
                 for q in range(4):
                     cc = 1 - c if q % 2 else c
-                    if d == 0:
-                        piece = dev(b // 2, b % 2, 1 - x if q >= 2 else x, cc)
-                    else:
-                        piece = dev(b // 2, 1 - y if q >= 2 else y, b % 2, cc)
-                    vals = stage[slot, piece, 0:1, d * HALF * 128:(d + 1) * HALF * 128].astype(F32)
-                    dense[dslot, d, q, pl.ds(row, HALF)] = vals.reshape(HALF, 128).astype(BF16)
+                    vals = []
+                    for o in range(2):
+                        if d == 0:
+                            piece = dev(b, o, 1 - x if q >= 2 else x, cc)
+                        else:
+                            piece = dev(b, 1 - y if q >= 2 else y, o, cc)
+                        flat = stage[slot, piece, 0:1, d * HALF * 128:(d + 1) * HALF * 128].astype(F32)
+                        vals.append(flat.reshape(HALF, 128))
+                    dense[dslot, d, q, pl.ds(row, 2 * HALF)] = jnp.concatenate(vals, axis=0).astype(BF16)
             return carry
 
-        lax.fori_loop(0, 8, conv, 0)
+        lax.fori_loop(0, 4, conv, 0)
 
     def stage0(k):
         dslot = k % 4
         for q in (3, 2, 1):
             for d in range(2):
                 to = ((partner, xs, xo), (partner, ys, yo))[d][q - 1]
-                send(dense.at[dslot, d, q], rbuf(k, d, q - 1), s0_send.at[dslot], s0_recv.at[k], to)
+                send(dense.at[dslot, d, q], rbuf(k, d, q - 1), s0_send.at[dslot], s0_recv.at[k % SLOTS], to)
 
         @pl.when(k + 1 < CHUNKS)
         def _():
@@ -221,47 +228,48 @@
 
     def stage1(k):
         dslot = k % 4
-        wait(dense.at[dslot, :, pl.ds(1, 3)], s0_recv.at[k])
+        wait(dense.at[dslot, :, pl.ds(1, 3)], s0_recv.at[k % SLOTS])
         for d in range(2):
             def add(b, carry, d=d):
-                row = pl.multiple_of(b * HALF, 16)
-                tot = dense[dslot, d, 0, pl.ds(row, HALF)].astype(F32)
+                row = pl.multiple_of(b * 2 * HALF, 16)
+                tot = dense[dslot, d, 0, pl.ds(row, 2 * HALF)].astype(F32)
                 for j in range(3):
-                    off = pl.multiple_of(roff(k, d) + j * 8 * HALF + b * HALF, 16)
-                    tot = tot + pb[(*rpiece(k, d), pl.ds(off, HALF))].astype(F32)
-                pab[k, d, b % 2, b // 2] = tot[0:RAB]
-                pcd[k, d, b // 2, b % 2] = tot[RAB:HALF]
+                    off = pl.multiple_of(roff(k, d) + j * 8 * HALF + b * 2 * HALF, 16)
+                    tot = tot + pb[(*rpiece(k, d), pl.ds(off, 2 * HALF))].astype(F32)
+                for o in range(2):
+                    pab[k, d, o, b] = tot[o * HALF:o * HALF + RAB]
+                    pcd[k, d, b, o] = tot[o * HALF + RAB:(o + 1) * HALF]
                 return carry
-            lax.fori_loop(0, 8, add, 0)
-        send(pab.at[k, 0, 1 - y], er.at[k, 0], rs_send.at[k], er_recv.at[k], ys)
-        send(pab.at[k, 1, 1 - x], er.at[k, 1], rs_send.at[k], er_recv.at[k], xs)
+            lax.fori_loop(0, 4, add, 0)
+        send(pab.at[k, 0, 1 - y], er.at[k, 0], rs_send.at[k], er_recv.at[k % SLOTS], ys)
+        send(pab.at[k, 1, 1 - x], er.at[k, 1], rs_send.at[k], er_recv.at[k % SLOTS], xs)
         for d in range(2):
-            z_first(k, pcd.at[k, d], cdr.at[k, d], cd_recv.at[k, d])
+            z_first(k, pcd.at[k, d], cdr.at[k, d], cd_recv.at[k % SLOTS, d])
 
     def stage2(k):
         for d in range(2):
-            z_second(k, pcd.at[k, d], cdr.at[k, d], cd_recv.at[k, d])
-        wait(er.at[k], er_recv.at[k])
+            z_second(k, pcd.at[k, d], cdr.at[k, d], cd_recv.at[k % SLOTS, d])
+        wait(er.at[k], er_recv.at[k % SLOTS])
         for zz in range(4):
             abz[k, zz, 0] = pab[k, 0, y, zz] + er[k, 0, zz]
             abz[k, zz, 1] = pab[k, 1, x, zz] + er[k, 1, zz]
-        z_first(k, abz.at[k], abr.at[k], ab_recv.at[k])
+        z_first(k, abz.at[k], abr.at[k], ab_recv.at[k % SLOTS])
 
     def stage3(k):
         for d in range(2):
-            z_third(k, pcd.at[k, d], cdr.at[k, d], cd_recv.at[k, d])
-        z_second(k, abz.at[k], abr.at[k], ab_recv.at[k])
+            z_third(k, pcd.at[k, d], cdr.at[k, d], cd_recv.at[k % SLOTS, d])
+        z_second(k, abz.at[k], abr.at[k], ab_recv.at[k % SLOTS])
 
     def stage4(k):
         for d in range(2):
-            z_final(k, pcd.at[k, d], cdr.at[k, d], cd_recv.at[k, d])
-        send(pcd.at[k, 0, z, 1 - y], fr.at[k, 0], rs_send.at[k], f_recv.at[k], ys)
-        send(pcd.at[k, 1, z, 1 - x], fr.at[k, 1], rs_send.at[k], f_recv.at[k], xs)
-        z_third(k, abz.at[k], abr.at[k], ab_recv.at[k])
+            z_final(k, pcd.at[k, d], cdr.at[k, d], cd_recv.at[k % SLOTS, d])
+        send(pcd.at[k, 0, z, 1 - y], fr.at[k, 0], rs_send.at[k], f_recv.at[k % SLOTS], ys)
+        send(pcd.at[k, 1, z, 1 - x], fr.at[k, 1], rs_send.at[k], f_recv.at[k % SLOTS], xs)
+        z_third(k, abz.at[k], abr.at[k], ab_recv.at[k % SLOTS])
 
     def stage5(k):
-        z_final(k, abz.at[k], abr.at[k], ab_recv.at[k])
-        wait(fr.at[k], f_recv.at[k])
+        z_final(k, abz.at[k], abr.at[k], ab_recv.at[k % SLOTS])
+        wait(fr.at[k], f_recv.at[k % SLOTS])
         base = pl.multiple_of(k * ROWS, 16)
         parts = (
             (0, RAB, abz[k, z, 0]),
@@ -284,7 +292,7 @@
             def _(fn=fn, k=k):
                 fn(k)
         for j in range(6):
-            @pl.when(i == 1 + 2 * j)
+            @pl.when(i == 4 + 4 * j)
             def _(j=j):
                 vec_step(j)
         return carry
@@ -307,9 +315,8 @@
     clip[...] = jnp.minimum(1.0, MAX_NORM / (jnp.sqrt(norm_sq) + NORM_EPS))
     rate = lr[0, 0]
 
-    wait(po, pmv_sem.at[0])
-    wait(mo, pmv_sem.at[1])
-    wait(vo, pmv_sem.at[2])
+    for i, (_, dst) in enumerate(loads[1:]):
+        wait(dst, pmv_sem.at[i + 1])
 
     def cut(k, off, num):
         return pl.ds(pl.multiple_of(k * AG_ROWS + off, 8), num)
@@ -403,12 +410,12 @@
 
     def ag0(k):
         def upd(b, carry):
-            rows = pl.ds(pl.multiple_of(k * AG_ROWS + b * 32, 16), 32)
+            rows = pl.ds(pl.multiple_of(k * AG_ROWS + b * 48, 16), 48)
             new = adam_update(gsum[rows] * clip[0:1], po[rows], mo[rows], vo[rows], rate, WEIGHT_DECAY)
             po[rows], mo[rows], vo[rows] = new
             pb[z, y, x, c, rows] = new[0].astype(BF16)
             return carry
-        lax.fori_loop(0, AG_ROWS // 32, upd, 0)
+        lax.fori_loop(0, AG_ROWS // 48, upd, 0)
         rc, rd = rows_of(k)[2:]
         push(region(z, y, x, rc), k, ag_cd1.at[k], ys)
         push(region(z, y, x, rd), k, ag_cd1.at[k], xs)
@@ -427,17 +434,17 @@
         push(region(full, full, full, cut(k, 0, AG_ROWS)), k, ag_d2d.at[k], partner)
 
     def ag_iter(i, carry):
-        for s, fn in enumerate((ag0, middle(1), middle(2), middle(3), middle(4), ag5)):
-            k = i - SKEW_AG * s
+        for s, fn in zip(AG_STAGES, (ag0, middle(1), middle(2), middle(3), middle(4), ag5)):
+            k = i - s
 
             @pl.when((k >= 0) & (k < AG_CHUNKS))
             def _(fn=fn, k=k):
                 fn(k)
         return carry
 
-    lax.fori_loop(0, AG_CHUNKS + 5 * SKEW_AG, ag_iter, 0)
-
-    newv = adam_update(gvec * clip[0:1], pv[...], mv[...], vv[...], rate, 0.0)
+    lax.fori_loop(0, AG_CHUNKS + AG_STAGES[-1], ag_iter, 0)
+
+    newv = adam_update(gvec * clip[0:1], pvo[...], mvo[...], vvo[...], rate, 0.0)
     pvo[...], mvo[...], vvo[...] = newv
 
     def drain_rs(k, carry):
@@ -454,7 +461,7 @@
 
         @pl.when(jnp.logical_not(mid))
         def _():
-            wait(pb.at[0, 0, 0, full, pl.ds(0, (base + along) // 2)], ag_send.at[k])
+            wait(pb.at[0, 0, full, full, pl.ds(0, (base + along) // 4)], ag_send.at[k])
 
         return carry
 
@@ -492,9 +499,10 @@
             + [pltpu.VMEM((VEC, 128), F32)] * 3
             + [pltpu.VMEM((4, 2, 2, 2, PIECE, 128), BF16)]
         ),
-        in_specs=[hbm, vm, hbm, hbm, hbm, vm, vm, vm, pl.BlockSpec(memory_space=pltpu.SMEM)],
+        in_specs=[hbm] * 8 + [pl.BlockSpec(memory_space=pltpu.SMEM)],
         out_specs=[vm] * 7,
         scratch_shapes=[
+            pltpu.VMEM((1, VEC * 128), BF16),
             pltpu.VMEM((2, DP, 1, ROWS * 128), BF16),
             pltpu.VMEM((4, 2, 4, 8 * HALF, 128), BF16),
             pltpu.VMEM((K, 2, 2, 4, RAB, 128), F32),
@@ -511,7 +519,7 @@
             pltpu.VMEM((5, VPAD, 128), F32),
             pltpu.VMEM((1, 128), F32),
             pltpu.VMEM((DP, 1, 128), F32),
-            dma((2,)), dma((3,)), dma((4,)), dma((K,)), dma((K,)), dma((K,)), dma((K, 2, 2)), dma((K, 2)), dma((K,)),
+            dma((2,)), dma((7,)), dma((4,)), dma((SLOTS,)), dma((K,)), dma((SLOTS,)), dma((SLOTS, 2, 2)), dma((SLOTS, 2)), dma((SLOTS,)),
             dma((5,)), dma((5,)), dma, dma,
             dma((G,)), dma((G, 2, 3)), dma((G, 2, 3)), dma((G,)), dma((G, 4)), dma((G,)), dma((G,)),
         ],

time: 255 us -> 245 us (0.961)
  Pallas kernels: 254 us -> 243 us
    pallas_call x1, Pallas kernels: 246 us -> 235 us  [local_step(): call(g_mat, g_vec, p_mat.reshape(PIECE, 128), m_mat.reshape(PIECE, 128),...]
where the time goes in v7:
time: 245 us
  Pallas kernels  243 us (99%)
    pallas_call x1, Pallas kernels, local_step(): call(g_mat, g_vec, p_mat.reshape(PIECE, 128), m_mat.reshape(PIECE, 128),...  235 us
    pallas_call x1, Pallas kernels, local_step(): return tuple((o.reshape(-1) for o in copy_out(*outs)))  7.96 us

profile of v7, /device:TPU:0, one launch (start us, length us, event | category | flops | bytes accessed | tf_op | source)
XLA Modules:
  0.0 244.6 jit_solution(1356714351934556769)
XLA Ops:
  1.3 235.4 %adam_step.1 = (f32[2400,128]{1,0:T(8,128)S(1)}, f32[2400,128]{1,0:T(8,128)S(1)}, f32[2400,128]{1,0:T(8,128)S(1)}, f32[130,128]{1,0:T(8,128)S(1)}, f32[130,128]{...) custom-call(bf16[1,9830400]{1,0:T(2,128)(2,1)} %g.1, bf16[1,16640]{1,0:T(2,128)(2,1)} %gv.1, ...), custom_call_target="tpu_custom_call" | custom-call | tf_op jit(solution)/shard_map/adam_step/pallas_call | solution.py:543
  236.6 8.0 %copy_out.1 = (f32[2400,128]{1,0:T(8,128)}, f32[2400,128]{1,0:T(8,128)}, f32[2400,128]{1,0:T(8,128)}, f32[130,128]{1,0:T(8,128)}, f32[130,128]{1,0:T(8,128)}, /*...) custom-call(f32[2400,128]{1,0:T(8,128)S(1)} %get-tuple-element.21.refs_0_, ...), custom_call_target="tpu_custom_call" | custom-call | tf_op jit(solution)/shard_map/copy_out/pallas_call | solution.py:549

commit v8 on v7

--- a/solution.py
+++ b/solution.py
@@ -85,8 +85,6 @@
             return carry
         lax.fori_loop(0, DP, one, 0)
 
-    fetch(0, 0)
-
     barrier = pltpu.get_barrier_semaphore()
     for nb in (partner, xs, xo, ys, yo, z2):
         pl.semaphore_signal(barrier, inc=1, device_id=(nb,), device_id_type=MESH)
@@ -99,6 +97,7 @@
     def _():
         pl.semaphore_signal(barrier, inc=1, device_id=(down,), device_id_type=MESH)
 
+    fetch(0, 0)
     ssq[...] = jnp.zeros((8, 128), F32)
 
     mid = (z >= 1) & (z <= 2)
@@ -145,10 +144,6 @@
     def convert(k):
         slot = k % 2
         dslot = k % 4
-
-        @pl.when(k + 1 < CHUNKS)
-        def _():
-            fetch(k + 1, 1 - slot)
 
         @pl.when(k >= 4)
         def _():
@@ -173,6 +168,10 @@
             return carry
 
         lax.fori_loop(0, 4, conv, 0)
+
+        @pl.when(k + 1 < CHUNKS)
+        def _():
+            fetch(k + 1, 1 - slot)
 
     def stage0(k):
         dslot = k % 4
@@ -430,8 +429,14 @@
         return fn
 
     def ag5(k):
-        wait(pb.at[0, full, full, full, cut(k, 0, AG_ROWS)], ag_h3.at[k])
-        push(region(full, full, full, cut(k, 0, AG_ROWS)), k, ag_d2d.at[k], partner)
+        ra, rb, rc, rd = rows_of(k)
+        for xx, yy in ((x, y), (1 - x, 1 - y)):
+            if xx is not x:
+                wait(pb.at[0, full, full, full, cut(k, 0, AG_ROWS)], ag_h3.at[k])
+            push(region(full, full, xx, ra), k, ag_d2d.at[k], partner)
+            push(region(full, yy, full, rb), k, ag_d2d.at[k], partner)
+            push(region(full, full, xx, rc), k, ag_d2d.at[k], partner)
+            push(region(full, yy, full, rd), k, ag_d2d.at[k], partner)
 
     def ag_iter(i, carry):
         for s, fn in zip(AG_STAGES, (ag0, middle(1), middle(2), middle(3), middle(4), ag5)):
@@ -476,7 +481,10 @@
 
 def finish(*refs):
     srcs, dsts, sem = refs[:7], refs[7:14], refs[14]
-    copies = [pltpu.make_async_copy(srcs[6].at[zz, yy], dsts[6].at[zz, yy], sem.at[6 + zz * 2 + yy]) for zz in range(4) for yy in range(2)]
+    copies = [
+        pltpu.make_async_copy(srcs[6].at[i // 4, i // 2 % 2, i % 2], dsts[6].at[i // 4, i // 2 % 2, i % 2], sem.at[6 + i])
+        for i in range(16)
+    ]
     copies += [pltpu.make_async_copy(srcs[i], dsts[i], sem.at[i]) for i in range(6)]
     for copy in copies:
         copy.start()
@@ -535,7 +543,7 @@
         out_shape=[jax.ShapeDtypeStruct(s, F32) for s in shapes] + [jax.ShapeDtypeStruct((4, 2, 2, 2, PIECE, 128), BF16)],
         in_specs=[vm] * 7,
         out_specs=[hbm] * 7,
-        scratch_shapes=[dma((14,))],
+        scratch_shapes=[dma((22,))],
         compiler_params=pltpu.CompilerParams(vmem_limit_bytes=2 ** 20),
     )
 

time: 245 us -> 244 us (level)
  no operation moved by 1% of the time
where the time goes in v8:
time: 244 us
  Pallas kernels  243 us (100%)
    pallas_call x1, Pallas kernels, local_step(): call(g_mat, g_vec, p_mat.reshape(PIECE, 128), m_mat.reshape(PIECE, 128),...  235 us
    pallas_call x1, Pallas kernels, local_step(): return tuple((o.reshape(-1) for o in copy_out(*outs)))  8.03 us

profile of v8, /device:TPU:0, one launch (start us, length us, event | category | flops | bytes accessed | tf_op | source)
XLA Modules:
  0.0 243.9 jit_solution(12106217205735222664)
XLA Ops:
  1.3 234.6 %adam_step.1 = (f32[2400,128]{1,0:T(8,128)S(1)}, f32[2400,128]{1,0:T(8,128)S(1)}, f32[2400,128]{1,0:T(8,128)S(1)}, f32[130,128]{1,0:T(8,128)S(1)}, f32[130,128]{...) custom-call(bf16[1,9830400]{1,0:T(2,128)(2,1)} %g.1, bf16[1,16640]{1,0:T(2,128)(2,1)} %gv.1, ...), custom_call_target="tpu_custom_call" | custom-call | tf_op jit(solution)/shard_map/adam_step/pallas_call | solution.py:551
  235.9 8.0 %copy_out.1 = (f32[2400,128]{1,0:T(8,128)}, f32[2400,128]{1,0:T(8,128)}, f32[2400,128]{1,0:T(8,128)}, f32[130,128]{1,0:T(8,128)}, f32[130,128]{1,0:T(8,128)}, /*...) custom-call(f32[2400,128]{1,0:T(8,128)S(1)} %get-tuple-element.21.refs_0_, ...), custom_call_target="tpu_custom_call" | custom-call | tf_op jit(solution)/shard_map/copy_out/pallas_call | solution.py:557

commit v9 on v8

--- a/solution.py
+++ b/solution.py
@@ -28,7 +28,7 @@
 RCD = HALF - RAB
 SKEW_RS = 2
 AG_STAGES = (0, 2, 3, 4, 5, 6)
-SLOTS = 16
+SLOTS = 12
 VEC = 130
 VPAD = 136
 MESH = pl.DeviceIdType.MESH
@@ -45,7 +45,7 @@
 
 def kernel(g, gv, p, m, v, pv, mv, vv, lr,
            po, mo, vo, pvo, mvo, vvo, pb,
-           gvb, stage, dense, pab, pcd, abz, er, cdr, abr, fr, gsum, ssq, clip, vs, vr, ns, nr,
+           lrs, gvb, stage, dense, pab, pcd, abz, er, cdr, abr, fr, gsum, ssq, clip, vs, vr, ns, nr,
            in_sem, pmv_sem, s0_send, s0_recv, rs_send, er_recv, cd_recv, ab_recv, f_recv,
            vec_send, vec_recv, norm_send, norm_recv,
            ag_send, ag_ab, ag_cd, ag_cd1, ag_h2, ag_h3, ag_d2d):
@@ -113,7 +113,7 @@
 
     partners = (partner, xs, ys, z1, z2)
 
-    loads = ((gv, gvb), (p, po), (m, mo), (v, vo), (pv, pvo), (mv, mvo), (vv, vvo))
+    loads = ((gv, gvb), (p, po), (m, mo), (v, vo), (pv, pvo), (mv, mvo), (vv, vvo), (lr, lrs))
 
     def vec_step(j):
         if j == 0:
@@ -300,6 +300,8 @@
     await_neighbours()
     lax.fori_loop(0, CHUNKS + 5 * SKEW_RS, rs_iter, 0)
 
+    for i, (src, dst) in enumerate(loads[1:]):
+        pltpu.make_async_copy(src, dst, pmv_sem.at[i + 1]).wait()
     ns[...] = jnp.sum(ssq[...], axis=0, keepdims=True)
     nr[me] = ns[...]
 
@@ -308,14 +310,13 @@
         return carry
 
     lax.fori_loop(1, DP, tell, 0)
+    gvec = vs[5, 0:VEC] * (1.0 / DP)
+    ssq[0:1] = jnp.sum(gvec * gvec, axis=0, keepdims=True)
     wait(nr.at[pl.ds(0, DP - 1)], norm_recv)
-    gvec = vs[5, 0:VEC] * (1.0 / DP)
-    norm_sq = jnp.full((8, 128), jnp.sum(nr[...]) + jnp.sum(gvec * gvec))
+    norm_sq = jnp.full((8, 128), jnp.sum(jnp.sum(nr[...], axis=0) + ssq[0:1]))
     clip[...] = jnp.minimum(1.0, MAX_NORM / (jnp.sqrt(norm_sq) + NORM_EPS))
-    rate = lr[0, 0]
-
-    for i, (_, dst) in enumerate(loads[1:]):
-        wait(dst, pmv_sem.at[i + 1])
+
+    rate = lrs[0, 0]
 
     def cut(k, off, num):
         return pl.ds(pl.multiple_of(k * AG_ROWS + off, 8), num)
@@ -371,8 +372,8 @@
 
         def fn(zz, side):
             if dist:
-                wait(region(0, 0, 0, ab), ag_ab.at[k, side, dist - 1])
-            onward_z(side, dist, lambda way, to: push(region(zz, y, x, ab), k, ag_ab.at[k, way, dist], to))
+                wait(region(0, 0, 0, ab), ag_ab.at[k, zz])
+            onward_z(side, dist, lambda way, to: push(region(zz, y, x, ab), k, ag_ab.at[k, zz], to))
             push(region(zz, y, x, ra), k, ag_h2.at[k, zz], ys)
             push(region(zz, y, x, rb), k, ag_h2.at[k, zz], xs)
 
@@ -395,11 +396,11 @@
             if dist == 0:
                 wait(region(0, 0, 0, cut(k, 0, 2 * AG_CD)), ag_cd1.at[k])
             else:
-                wait(pb.at[0, 0, full, full, rc], ag_cd.at[k, side, dist - 1])
+                wait(pb.at[0, 0, full, full, rc], ag_cd.at[k, zz])
 
             def on(way, to):
-                push(region(zz, full, x, rc), k, ag_cd.at[k, way, dist], to)
-                push(region(zz, y, full, rd), k, ag_cd.at[k, way, dist], to)
+                push(region(zz, full, x, rc), k, ag_cd.at[k, zz], to)
+                push(region(zz, y, full, rd), k, ag_cd.at[k, zz], to)
 
             onward_z(side, dist, on)
             push(region(zz, full, x, rc), k, ag_h3.at[k], xs)
@@ -507,9 +508,10 @@
             + [pltpu.VMEM((VEC, 128), F32)] * 3
             + [pltpu.VMEM((4, 2, 2, 2, PIECE, 128), BF16)]
         ),
-        in_specs=[hbm] * 8 + [pl.BlockSpec(memory_space=pltpu.SMEM)],
+        in_specs=[hbm] * 9,
         out_specs=[vm] * 7,
         scratch_shapes=[
+            pltpu.SMEM((1, 1), F32),
             pltpu.VMEM((1, VEC * 128), BF16),
             pltpu.VMEM((2, DP, 1, ROWS * 128), BF16),
             pltpu.VMEM((4, 2, 4, 8 * HALF, 128), BF16),
@@ -527,9 +529,9 @@
             pltpu.VMEM((5, VPAD, 128), F32),
             pltpu.VMEM((1, 128), F32),
             pltpu.VMEM((DP, 1, 128), F32),
-            dma((2,)), dma((7,)), dma((4,)), dma((SLOTS,)), dma((K,)), dma((SLOTS,)), dma((SLOTS, 2, 2)), dma((SLOTS, 2)), dma((SLOTS,)),
+            dma((2,)), dma((8,)), dma((4,)), dma((SLOTS,)), dma((K,)), dma((SLOTS,)), dma((SLOTS, 2, 2)), dma((SLOTS, 2)), dma((SLOTS,)),
             dma((5,)), dma((5,)), dma, dma,
-            dma((G,)), dma((G, 2, 3)), dma((G, 2, 3)), dma((G,)), dma((G, 4)), dma((G,)), dma((G,)),
+            dma((G,)), dma((G, 4)), dma((G, 4)), dma((G,)), dma((G, 4)), dma((G,)), dma((G,)),
         ],
         compiler_params=pltpu.CompilerParams(
             collective_id=0, has_side_effects=True, vmem_limit_bytes=37 * 2 ** 20

time: 244 us -> 244 us (level)
  no operation moved by 1% of the time
where the time goes in v9:
time: 244 us; the launch traced here: 243 us
  Pallas kernels  242 us (99%)
    pallas_call x1, Pallas kernels, local_step(): call(g_mat, g_vec, p_mat.reshape(PIECE, 128), m_mat.reshape(PIECE, 128),...  234 us
    pallas_call x1, Pallas kernels, local_step(): return tuple((o.reshape(-1) for o in copy_out(*outs)))  8.03 us

profile of v9, /device:TPU:0, one launch (start us, length us, event | category | flops | bytes accessed | tf_op | source)
XLA Modules:
  0.0 243.3 jit_solution(10500889700467190738)
XLA Ops:
  1.3 233.9 %adam_step.1 = (f32[2400,128]{1,0:T(8,128)S(1)}, f32[2400,128]{1,0:T(8,128)S(1)}, f32[2400,128]{1,0:T(8,128)S(1)}, f32[130,128]{1,0:T(8,128)S(1)}, f32[130,128]{...) custom-call(bf16[1,9830400]{1,0:T(2,128)(2,1)} %g.1, bf16[1,16640]{1,0:T(2,128)(2,1)} %gv.1, ...), custom_call_target="tpu_custom_call" | custom-call | tf_op jit(solution)/shard_map/adam_step/pallas_call | solution.py:553
  235.2 8.0 %copy_out.1 = (f32[2400,128]{1,0:T(8,128)}, f32[2400,128]{1,0:T(8,128)}, f32[2400,128]{1,0:T(8,128)}, f32[130,128]{1,0:T(8,128)}, f32[130,128]{1,0:T(8,128)}, /*...) custom-call(f32[2400,128]{1,0:T(8,128)S(1)} %get-tuple-element.21.refs_0_, ...), custom_call_target="tpu_custom_call" | custom-call | tf_op jit(solution)/shard_map/copy_out/pallas_call | solution.py:559

commit v10 on v9

--- a/solution.py
+++ b/solution.py
@@ -384,8 +384,8 @@
 
         def fn(zz, side):
             wait(region(0, 0, 0, cut(k, 0, 2 * AG_AB)), ag_h2.at[k, zz])
-            push(region(zz, full, x, ra), k, ag_h3.at[k], xs)
-            push(region(zz, y, full, rb), k, ag_h3.at[k], ys)
+            push(region(zz, full, x, ra), k, ag_h3.at[k, zz], xs)
+            push(region(zz, y, full, rb), k, ag_h3.at[k, zz], ys)
 
         sides(dist, fn)
 
@@ -403,8 +403,8 @@
                 push(region(zz, y, full, rd), k, ag_cd.at[k, zz], to)
 
             onward_z(side, dist, on)
-            push(region(zz, full, x, rc), k, ag_h3.at[k], xs)
-            push(region(zz, y, full, rd), k, ag_h3.at[k], ys)
+            push(region(zz, full, x, rc), k, ag_h3.at[k, zz], xs)
+            push(region(zz, y, full, rd), k, ag_h3.at[k, zz], ys)
 
         sides(dist, fn)
 
@@ -415,10 +415,11 @@
             po[rows], mo[rows], vo[rows] = new
             pb[z, y, x, c, rows] = new[0].astype(BF16)
             return carry
-        lax.fori_loop(0, AG_ROWS // 48, upd, 0)
+        lax.fori_loop(2 * AG_AB // 48, AG_ROWS // 48, upd, 0)
         rc, rd = rows_of(k)[2:]
         push(region(z, y, x, rc), k, ag_cd1.at[k], ys)
         push(region(z, y, x, rd), k, ag_cd1.at[k], xs)
+        lax.fori_loop(0, 2 * AG_AB // 48, upd, 0)
         ab_arrived(k, 0)
 
     def middle(s):
@@ -431,13 +432,20 @@
 
     def ag5(k):
         ra, rb, rc, rd = rows_of(k)
-        for xx, yy in ((x, y), (1 - x, 1 - y)):
-            if xx is not x:
-                wait(pb.at[0, full, full, full, cut(k, 0, AG_ROWS)], ag_h3.at[k])
-            push(region(full, full, xx, ra), k, ag_d2d.at[k], partner)
-            push(region(full, yy, full, rb), k, ag_d2d.at[k], partner)
-            push(region(full, full, xx, rc), k, ag_d2d.at[k], partner)
-            push(region(full, yy, full, rd), k, ag_d2d.at[k], partner)
+
+        def over(zz, xx, yy):
+            push(region(zz, full, xx, ra), k, ag_d2d.at[k], partner)
+            push(region(zz, yy, full, rb), k, ag_d2d.at[k], partner)
+            push(region(zz, full, xx, rc), k, ag_d2d.at[k], partner)
+            push(region(zz, yy, full, rd), k, ag_d2d.at[k], partner)
+
+        def fn(zz, side):
+            wait(pb.at[0, 0, 0, full, cut(k, 0, AG_ROWS)], ag_h3.at[k, zz])
+            over(zz, 1 - x, 1 - y)
+
+        over(full, x, y)
+        for dist in range(4):
+            sides(dist, fn)
 
     def ag_iter(i, carry):
         for s, fn in zip(AG_STAGES, (ag0, middle(1), middle(2), middle(3), middle(4), ag5)):
@@ -531,7 +539,7 @@
             pltpu.VMEM((DP, 1, 128), F32),
             dma((2,)), dma((8,)), dma((4,)), dma((SLOTS,)), dma((K,)), dma((SLOTS,)), dma((SLOTS, 2, 2)), dma((SLOTS, 2)), dma((SLOTS,)),
             dma((5,)), dma((5,)), dma, dma,
-            dma((G,)), dma((G, 4)), dma((G, 4)), dma((G,)), dma((G, 4)), dma((G,)), dma((G,)),
+            dma((G,)), dma((G, 4)), dma((G, 4)), dma((G,)), dma((G, 4)), dma((G, 4)), dma((G,)),
         ],
         compiler_params=pltpu.CompilerParams(
             collective_id=0, has_side_effects=True, vmem_limit_bytes=37 * 2 ** 20

time: 244 us -> 243 us (level)
  no operation moved by 1% of the time
where the time goes in v10:
time: 243 us
  Pallas kernels  242 us (100%)
    pallas_call x1, Pallas kernels, local_step(): call(g_mat, g_vec, p_mat.reshape(PIECE, 128), m_mat.reshape(PIECE, 128),...  234 us
    pallas_call x1, Pallas kernels, local_step(): return tuple((o.reshape(-1) for o in copy_out(*outs)))  8.03 us

profile of v10, /device:TPU:0, one launch (start us, length us, event | category | flops | bytes accessed | tf_op | source)
XLA Modules:
  0.0 242.9 jit_solution(1501342569929929347)
XLA Ops:
  1.3 233.6 %adam_step.1 = (f32[2400,128]{1,0:T(8,128)S(1)}, f32[2400,128]{1,0:T(8,128)S(1)}, f32[2400,128]{1,0:T(8,128)S(1)}, f32[130,128]{1,0:T(8,128)S(1)}, f32[130,128]{...) custom-call(bf16[1,9830400]{1,0:T(2,128)(2,1)} %g.1, bf16[1,16640]{1,0:T(2,128)(2,1)} %gv.1, ...), custom_call_target="tpu_custom_call" | custom-call | tf_op jit(solution)/shard_map/adam_step/pallas_call | solution.py:561
  234.9 8.0 %copy_out.1 = (f32[2400,128]{1,0:T(8,128)}, f32[2400,128]{1,0:T(8,128)}, f32[2400,128]{1,0:T(8,128)}, f32[130,128]{1,0:T(8,128)}, f32[130,128]{1,0:T(8,128)}, /*...) custom-call(f32[2400,128]{1,0:T(8,128)S(1)} %get-tuple-element.21.refs_0_, ...), custom_call_target="tpu_custom_call" | custom-call | tf_op jit(solution)/shard_map/copy_out/pallas_call | solution.py:567

commit v11 on v10

--- a/solution.py
+++ b/solution.py
@@ -26,9 +26,9 @@
 HALF = ROWS // 2
 RAB = 8
 RCD = HALF - RAB
-SKEW_RS = 2
+SKEW_RS = 3
 AG_STAGES = (0, 2, 3, 4, 5, 6)
-SLOTS = 12
+SLOTS = 20
 VEC = 130
 VPAD = 136
 MESH = pl.DeviceIdType.MESH
@@ -143,9 +143,9 @@
 
     def convert(k):
         slot = k % 2
-        dslot = k % 4
-
-        @pl.when(k >= 4)
+        dslot = k % 5
+
+        @pl.when(k >= 5)
         def _():
             wait(dense.at[dslot, :, pl.ds(1, 3)], s0_send.at[dslot])
 
@@ -174,7 +174,7 @@
             fetch(k + 1, 1 - slot)
 
     def stage0(k):
-        dslot = k % 4
+        dslot = k % 5
         for q in (3, 2, 1):
             for d in range(2):
                 to = ((partner, xs, xo), (partner, ys, yo))[d][q - 1]
@@ -226,7 +226,7 @@
             bufs[z] += recv[0]
 
     def stage1(k):
-        dslot = k % 4
+        dslot = k % 5
         wait(dense.at[dslot, :, pl.ds(1, 3)], s0_recv.at[k % SLOTS])
         for d in range(2):
             def add(b, carry, d=d):
@@ -481,7 +481,7 @@
 
     lax.fori_loop(0, CHUNKS, drain_rs, 0)
     lax.fori_loop(0, AG_CHUNKS, drain_ag, 0)
-    for s in range(4):
+    for s in range(5):
         wait(dense.at[s, :, pl.ds(1, 3)], s0_send.at[s])
     for j in range(5):
         wait(vs.at[j], vec_send.at[j])
@@ -491,8 +491,8 @@
 def finish(*refs):
     srcs, dsts, sem = refs[:7], refs[7:14], refs[14]
     copies = [
-        pltpu.make_async_copy(srcs[6].at[i // 4, i // 2 % 2, i % 2], dsts[6].at[i // 4, i // 2 % 2, i % 2], sem.at[6 + i])
-        for i in range(16)
+        pltpu.make_async_copy(srcs[6].at[i // 2, i % 2], dsts[6].at[i // 2, i % 2], sem.at[6 + i])
+        for i in range(8)
     ]
     copies += [pltpu.make_async_copy(srcs[i], dsts[i], sem.at[i]) for i in range(6)]
     for copy in copies:
@@ -522,7 +522,7 @@
             pltpu.SMEM((1, 1), F32),
             pltpu.VMEM((1, VEC * 128), BF16),
             pltpu.VMEM((2, DP, 1, ROWS * 128), BF16),
-            pltpu.VMEM((4, 2, 4, 8 * HALF, 128), BF16),
+            pltpu.VMEM((5, 2, 4, 8 * HALF, 128), BF16),
             pltpu.VMEM((K, 2, 2, 4, RAB, 128), F32),
             pltpu.VMEM((K, 2, 4, 2, RCD, 128), F32),
             pltpu.VMEM((K, 4, 2, RAB, 128), F32),
@@ -537,7 +537,7 @@
             pltpu.VMEM((5, VPAD, 128), F32),
             pltpu.VMEM((1, 128), F32),
             pltpu.VMEM((DP, 1, 128), F32),
-            dma((2,)), dma((8,)), dma((4,)), dma((SLOTS,)), dma((K,)), dma((SLOTS,)), dma((SLOTS, 2, 2)), dma((SLOTS, 2)), dma((SLOTS,)),
+            dma((2,)), dma((8,)), dma((5,)), dma((SLOTS,)), dma((K,)), dma((SLOTS,)), dma((SLOTS, 2, 2)), dma((SLOTS, 2)), dma((SLOTS,)),
             dma((5,)), dma((5,)), dma, dma,
             dma((G,)), dma((G, 4)), dma((G, 4)), dma((G,)), dma((G, 4)), dma((G, 4)), dma((G,)),
         ],
@@ -553,7 +553,7 @@
         out_shape=[jax.ShapeDtypeStruct(s, F32) for s in shapes] + [jax.ShapeDtypeStruct((4, 2, 2, 2, PIECE, 128), BF16)],
         in_specs=[vm] * 7,
         out_specs=[hbm] * 7,
-        scratch_shapes=[dma((22,))],
+        scratch_shapes=[dma((14,))],
         compiler_params=pltpu.CompilerParams(vmem_limit_bytes=2 ** 20),
     )
 

time: 243 us -> 245 us (level)
  no operation moved by 1% of the time
where the time goes in v11:
time: 245 us; the launch traced here: 244 us
  Pallas kernels  243 us (99%)
    pallas_call x1, Pallas kernels, local_step(): call(g_mat, g_vec, p_mat.reshape(PIECE, 128), m_mat.reshape(PIECE, 128),...  235 us
    pallas_call x1, Pallas kernels, local_step(): return tuple((o.reshape(-1) for o in copy_out(*outs)))  7.96 us

profile of v11, /device:TPU:0, one launch (start us, length us, event | category | flops | bytes accessed | tf_op | source)
XLA Modules:
  0.0 244.0 jit_solution(5886060221034628698)
XLA Ops:
  1.3 234.7 %adam_step.1 = (f32[2400,128]{1,0:T(8,128)S(1)}, f32[2400,128]{1,0:T(8,128)S(1)}, f32[2400,128]{1,0:T(8,128)S(1)}, f32[130,128]{1,0:T(8,128)S(1)}, f32[130,128]{...) custom-call(bf16[1,9830400]{1,0:T(2,128)(2,1)} %g.1, bf16[1,16640]{1,0:T(2,128)(2,1)} %gv.1, ...), custom_call_target="tpu_custom_call" | custom-call | tf_op jit(solution)/shard_map/adam_step/pallas_call | solution.py:561
  236.0 8.0 %copy_out.1 = (f32[2400,128]{1,0:T(8,128)}, f32[2400,128]{1,0:T(8,128)}, f32[2400,128]{1,0:T(8,128)}, f32[130,128]{1,0:T(8,128)}, f32[130,128]{1,0:T(8,128)}, /*...) custom-call(f32[2400,128]{1,0:T(8,128)S(1)} %get-tuple-element.21.refs_0_, ...), custom_call_target="tpu_custom_call" | custom-call | tf_op jit(solution)/shard_map/copy_out/pallas_call | solution.py:567
